TPU v7x, 32 devices: a whole 2x2x4 slice. The times are simulated.
32 devices in a mesh: groups: 2 (over y), ep: 8 (over z, core), tp: 2 (over x).
Axes of the slice: x: 2, y: 2, z: 4, core: 2. Of those that a mesh axis runs over, the one named last changes fastest.
Arguments:
- hidden: bfloat16 [1024, 2880], P(('groups', 'ep')), parts along dimension 0, may hold values from -6 to 6
- route_experts: int32 [1024, 4], P(('groups', 'ep')), parts along dimension 0, may hold values from 0 to 7, all different within a row; in each aligned block of 64 rows (0 to 63, 64 to 127, ...) at most 64 rows name the same one
- route_weight: float32 [1024, 4], P(('groups', 'ep')), parts along dimension 0, may hold values from 0.1 to 0.6
- norm_gain: bfloat16 [2880], replicated, may hold values from 0.099609375 to 1.8984375
- gate_up_codes: int32 [8, 360, 5120], P('ep', None, 'tp'), may hold values from -2147483648 to 2147483646
- gate_up_scales: bfloat16 [8, 90, 5120], P('ep', None, 'tp'), as said below
- gate_up_bias: bfloat16 [8, 5120], P('ep', 'tp'), may hold values from -3 to 3
- down_codes: int32 [8, 2560, 360], P('ep', 'tp'), may hold values from -2147483648 to 2147483646
- down_scales: bfloat16 [8, 80, 2880], P('ep', 'tp'), as said below
- down_bias: bfloat16 [8, 2880], P('ep', 'tp'), may hold values from -3 to 3
Outputs:
- layer_out: bfloat16 [1024, 2880], P(('groups', 'ep'), 'tp'), parts along dimension 0
There are 2 independent parts, one for each index of `groups`. A program takes and returns all parts, laid end to end along the dimension named above; an argument that names none is the same for every part. Nothing has to cross between parts.
Inputs may be any that keep to these rules, and one draw needn't show every extreme that they name: `route_experts`: each row names 4 different experts. In each aligned block of 64 rows no expert is named by more than 64 rows, and in some blocks one expert is named by exactly 64 rows. `gate_up_scales`: every scale is a power of two. `down_scales`: every scale is a power of two.
All inputs are finite; a program needn't handle non-finite values.
Results may differ from a plain program's by a relative error of at most 0.013.
Values may be sent and summed in bfloat16 or wider, within the bound.
No kernel may reach another device: no remote copies, remote signals or barrier semaphores. Data moves between devices by JAX's collectives and lax.ppermute only.
A program may use at most 128 MiB of HBM per device.

v0:
```python
import jax
import jax.numpy as jnp
from jax import lax
from jax.sharding import PartitionSpec as P


def decode_nibble(nibble):
    magnit = nibble & 7
    exponent = jnp.maximum(jnp.right_shift(magnit, 1) - 1, 0)
    doubled = jnp.where(magnit < 2, magnit, jnp.left_shift(2 + (magnit & 1), exponent))
    signed_val = doubled.astype(jnp.float32) * 0.5
    return jnp.where(nibble >= 8, -signed_val, signed_val)


def unpack_weights(packed, scaling):
    row_count = packed.shape[0]
    shifts = jnp.arange(8, dtype=jnp.int32) * 4
    nibble = jnp.right_shift(packed[:, :, None], shifts[None, None, :]) & 15
    nibble = nibble.reshape(row_count, packed.shape[1] * 8)
    signed_val = decode_nibble(nibble)
    signed_val = (
        signed_val.reshape(row_count // 32, 32, -1) * scaling.astype(jnp.float32)[:, None, :]
    )
    return signed_val.reshape(row_count, -1).astype(jnp.bfloat16)


def unpack_rows(packed, scaling):
    row_count = packed.shape[0] * 8
    shifts = jnp.arange(8, dtype=jnp.int32) * 4
    nibble = jnp.right_shift(packed[:, None, :], shifts[None, :, None]) & 15
    nibble = nibble.reshape(row_count, packed.shape[1])
    signed_val = decode_nibble(nibble)
    signed_val = (
        signed_val.reshape(row_count // 32, 32, -1) * scaling.astype(jnp.float32)[:, None, :]
    )
    return signed_val.reshape(row_count, -1).astype(jnp.bfloat16)


def rms_normed(hidden, norm_gain):
    widened = hidden.astype(jnp.float32)
    mean_square = jnp.mean(widened * widened, axis=-1, keepdims=True)
    scaled = widened * lax.rsqrt(mean_square + 1e-05) * norm_gain.astype(jnp.float32)
    return scaled.astype(jnp.bfloat16)


def shards(
    hidden,
    route_experts,
    route_weight,
    norm_gain,
    gate_up_codes,
    gate_up_scales,
    gate_up_bias,
    down_codes,
    down_scales,
    down_bias,
):
    ep_count = lax.axis_size("ep")
    tp_count = lax.axis_size("tp")
    tp_rank = lax.axis_index("tp")
    tok_count, model_width = hidden.shape
    top_count = route_experts.shape[1]
    capacity = min(tok_count, max(tp_count, 2 * tok_count * top_count // ep_count))
    normed = rms_normed(hidden, norm_gain)
    flat_routes = route_experts.reshape(-1)
    onehot = (flat_routes[:, None] == jnp.arange(ep_count, dtype=jnp.int32)[None, :]).astype(
        jnp.int32
    )
    before = jnp.cumsum(onehot, axis=0) - onehot
    slot_of = jnp.sum(before * onehot, axis=1)
    target = (flat_routes * capacity + slot_of).reshape(tok_count, top_count)
    columns = jnp.arange(ep_count * capacity, dtype=jnp.int32)
    matches = target[:, :, None] == columns[None, None, :]
    placing = jnp.any(matches, axis=1).astype(jnp.bfloat16)
    weighting = jnp.sum(jnp.where(matches, route_weight[:, :, None], 0.0), axis=1)
    outgoing = lax.dot_general(
        placing, normed, (((0,), (0,)), ((), ())), preferred_element_type=jnp.float32
    ).astype(jnp.bfloat16)
    outgoing = outgoing.reshape(ep_count, capacity, model_width)
    gate_up_weight = unpack_rows(gate_up_codes[0], gate_up_scales[0])
    down_weight = unpack_weights(down_codes[0], down_scales[0])
    arrived = lax.all_to_all(outgoing, "ep", split_axis=0, concat_axis=0, tiled=True)
    source_count, item_count, _ = arrived.shape
    flat_rows = arrived.reshape(source_count * item_count, model_width)
    projected = jnp.dot(
        flat_rows, gate_up_weight, preferred_element_type=jnp.float32
    ) + gate_up_bias[0].astype(jnp.float32)
    gate_part = jnp.minimum(projected[:, 0::2], 7.0)
    upward = jnp.clip(projected[:, 1::2], -7.0, 7.0)
    activated = (gate_part * jax.nn.sigmoid(1.702 * gate_part) * (upward + 1.0)).astype(
        jnp.bfloat16
    )
    partial_value = jnp.dot(activated, down_weight, preferred_element_type=jnp.float32)
    partial_value = partial_value.astype(jnp.bfloat16).astype(jnp.float32)
    partial_value = partial_value.reshape(source_count, item_count, model_width)
    summed = lax.psum_scatter(
        partial_value.astype(jnp.bfloat16), "tp", scatter_dimension=2, tiled=True
    ).astype(jnp.float32)
    answered = (summed + down_bias[0].astype(jnp.float32)).astype(jnp.bfloat16)
    came_back = lax.all_to_all(answered, "ep", split_axis=0, concat_axis=0, tiled=True)
    quarter = model_width // tp_count
    own_cols = lax.dynamic_slice_in_dim(hidden, tp_rank * quarter, quarter, 1).astype(jnp.float32)
    gathered = came_back.reshape(ep_count * capacity, quarter).astype(jnp.float32)
    layer_out = own_cols + jnp.dot(weighting, gathered, precision=lax.Precision.HIGHEST)
    return layer_out.astype(jnp.bfloat16)


def solution(mesh):
    placed = (
        P(("groups", "ep"), None),
        P(("groups", "ep"), None),
        P(("groups", "ep"), None),
        P(),
        P("ep", None, "tp"),
        P("ep", None, "tp"),
        P("ep", "tp"),
        P("ep", "tp", None),
        P("ep", "tp", None),
        P("ep", "tp"),
    )
    return jax.shard_map(
        shards, mesh=mesh, in_specs=placed, out_specs=P(("groups", "ep"), "tp"), check_vma=False
    )
```

profile of v0, /device:TPU:0, one launch (start us, length us, event | category | flops | bytes accessed | tf_op | source)
XLA Modules:
  0.0 424.5 jit_solution(15950444374108988437)
XLA Ops:
  6.5 0.8 copy.46
  7.3 0.1 eq.42
  7.4 0.1 eq.38
  7.5 0.6 reduce-window.6
  8.1 0.2 slice_reduce_fusion
  8.4 0.1 fusion.44
  8.5 0.1 reduce_sum.30
  8.6 0.1 copy.48
  8.7 0.7 multiply_add_fusion
  9.4 0.1 fusion.39
  9.5 0.7 convert_element_type.112
  10.2 1.2 fusion.36
  11.4 2.0 convolution_convert_fusion
  13.4 0.0 copy-start.2
  13.4 3.1 copy.49
  16.5 6.4 %all-to-all-start = ((bf16[8,64,2880]{2,1,0:T(8,128)(2,1)}), bf16[8,64,2880]{2,1,0:T(8,128)(2,1)S(1)}, u32[]{:S(2)}, u32[]{:S(2)}) async-start(bf16[8,64,2880]{2,1,0:T(8,128)(2,1)} %bitcast.93), calls=%async_computation | async-start | bytes 6029312 | tf_op jit(solution)/shard_map/all_to_all | solution.py:82
  22.9 0.2 reduce-scatter.4.cloned.1.call-start
  23.1 0.1 shift_right_arithmetic.76
  23.2 0.1 shift_right_arithmetic.84
  23.3 0.0 copy-done.2
  23.4 6.3 %mul.129 = f32[40,32,2880]{2,1,0:T(8,128)} broadcast(f32[40,2880]{1,0:T(8,128)S(1)} %bitcast_convert_fusion.1), dimensions={0,2} | broadcast | bytes 15206400 | tf_op jit(solution)/shard_map/mul | solution.py:22
  29.7 15.2 %copy.50 = f32[1280,2880]{0,1:T(8,128)} copy(f32[1280,2880]{1,0:T(8,128)} %bitcast.90) | data formatting | bytes 29491200 | tf_op jit(solution)/shard_map/mul | solution.py:22
  45.0 0.0 copy-done.3
  45.0 0.0 copy-done.1
  45.0 0.1 bitcast_convert_fusion
  45.1 6.5 %shift_right_arithmetic.73 = s32[360,8,2560]{2,1,0:T(8,128)S(1)} broadcast(s32[360,2560]{1,0:T(8,128)} %bitcast.97), dimensions={0,2} | broadcast | bytes 33177600 | tf_op jit(solution)/shard_map/shift_right_arithmetic | solution.py:30
  51.6 19.6 %fusion.1 = bf16[90,32,2560]{2,1,0:T(8,128)(2,1)} fusion(f32[90,2560]{1,0:T(8,128)S(1)} %bitcast_convert_fusion, s32[32]{0:T(128)S(1)} %shift_right_arithmetic.76, s32[90,32,2560]{2,1,0:T(8,128)S(1)} %bitcast.89), kind=kLoop, calls=%fused_computation.4 | loop fusion | flops 132710400 | bytes 45158528 | tf_op jit(solution)/shard_map/convert_element_type | solution.py:36
  71.2 20.4 %all-to-all-done = bf16[8,64,2880]{2,1,0:T(8,128)(2,1)S(1)} async-done(((bf16[8,64,2880]{2,1,0:T(8,128)(2,1)}), bf16[8,64,2880]{2,1,0:T(8,128)(2,1)S(1)}, u32[]{:S(2)}, u32[]{:S(2)}) %all-to-all-start) | async-done | bytes 2949152 | tf_op jit(solution)/shard_map/all_to_all | solution.py:82
  91.6 13.1 %convolution_add_fusion = f32[512,2560]{1,0:T(8,128)} fusion(bf16[512,2880]{1,0:T(8,128)(2,1)S(1)} %bitcast.98, bf16[2880,2560]{1,0:T(8,128)(2,1)} %bitcast.92, f32[2560]{0:T(1024)S(1)} %convert_reduce_fusion), kind=kOutput, calls=%fused_computation.33 | convolution fusion | flops 7551057920 | bytes 22947840 | tf_op jit(solution)/shard_map/dot_general | solution.py:85
  104.7 91.5 %slice.14 = f32[512,1280]{1,0:T(8,128)S(1)} slice(f32[512,2560]{1,0:T(8,128)} %convolution_add_fusion), slice={[0:512:1], [0:2560:2]} | slice | bytes 5242880 | tf_op jit(solution)/shard_map/slice | solution.py:88
  196.2 91.9 %slice.15 = f32[512,1280]{1,0:T(8,128)} slice(f32[512,2560]{1,0:T(8,128)} %convolution_add_fusion), slice={[0:512:1], [1:2560:2]} | slice | bytes 5242880 | tf_op jit(solution)/shard_map/slice | solution.py:89
  288.0 16.8 %fusion.28 = bf16[512,2880]{0,1:T(8,128)(2,1)} fusion(f32[1280,2880]{0,1:T(8,128)} %copy.50, s32[2880]{0:T(1024)S(1)} %shift_right_arithmetic.84, s32[1280,360]{0,1:T(8,128)} %bitcast.99, f32[512,1280]{1,0:T(8,128)} %slice.15, f32[512,1280]{1,0:T(8,128)S(1)} %slice.14), kind=kOutput, calls=%fused_computation.34 | convolution fusion | flops 3849256960 | bytes 24792320 | tf_op jit(solution)/shard_map/dot_general | solution.py:93
  304.8 3.3 copy.51
  308.2 6.0 %copy.52 = bf16[8,64,2880]{1,0,2:T(8,128)(2,1)} copy(bf16[8,64,2880]{2,1,0:T(8,128)(2,1)S(1)} %bitcast.94) | data formatting | bytes 5898240
  314.1 8.9 %reshape.147 = bf16[2880,512]{1,0:T(8,128)(2,1)} reshape(bf16[2880,8,64]{2,1,0:T(8,128)(2,1)} %bitcast.91) | data formatting | bytes 5898240
  323.0 0.0 reduce-scatter.4.cloned.1.call-update
  323.1 0.0 copy-done.4
  323.1 0.0 copy-start.5
  323.1 0.0 copy-start
  323.1 40.3 %reduce-scatter.4.cloned.1.call-done = bf16[1440,512]{1,0:T(8,128)(2,1)} async-done(((bf16[2880,512]{1,0:T(8,128)(2,1)}), bf16[1440,512]{1,0:T(8,128)(2,1)}) %reduce-scatter.4.cloned.1.call-update) | async-done | bytes 1474576
  363.4 3.8 reshape.148
  367.2 3.6 copy.53
  370.8 2.8 add_convert_fusion
  373.6 4.6 %all-to-all-start.1 = ((bf16[8,64,1440]{2,1,0:T(8,128)(2,1)}), bf16[8,64,1440]{2,1,0:T(8,128)(2,1)S(1)}, u32[]{:S(2)}, u32[]{:S(2)}) async-start(bf16[8,64,1440]{2,1,0:T(8,128)(2,1)} %add_convert_fusion), calls=%async_computation.1 | async-start | bytes 3145728 | tf_op jit(solution)/shard_map/all_to_all | solution.py:100
  378.3 0.0 copy-done.5
  378.3 0.1 select_reduce_fusion
  378.4 37.7 %all-to-all-done.1 = bf16[8,64,1440]{2,1,0:T(8,128)(2,1)S(1)} async-done(((bf16[8,64,1440]{2,1,0:T(8,128)(2,1)}), bf16[8,64,1440]{2,1,0:T(8,128)(2,1)S(1)}, u32[]{:S(2)}, u32[]{:S(2)}) %all-to-all-start.1) | async-done | bytes 1474592 | tf_op jit(solution)/shard_map/all_to_all | solution.py:100
  416.1 1.6 fusion.31
  (14 shorter events, 0.2 us)
Async XLA Ops:
  13.4 9.9 %copy-start.2 = (bf16[1,40,2880]{2,1,0:T(8,128)(2,1)S(1)}, bf16[1,40,2880]{2,1,0:T(8,128)(2,1)}, u32[]{:S(2)}) copy-start(bf16[1,40,2880]{2,1,0:T(8,128)(2,1)} %param.18) | copy-start | bytes 691204
  16.5 75.0 %all-to-all-start = ((bf16[8,64,2880]{2,1,0:T(8,128)(2,1)}), bf16[8,64,2880]{2,1,0:T(8,128)(2,1)S(1)}, u32[]{:S(2)}, u32[]{:S(2)}) async-start(bf16[8,64,2880]{2,1,0:T(8,128)(2,1)} %bitcast.93), calls=%async_computation | async-start | bytes 6029312 | tf_op jit(solution)/shard_map/all_to_all | solution.py:82
  22.9 340.5 %reduce-scatter.4.cloned.1.call-start = ((), (), s32[]{:S(2)}) async-start(), calls=%async_computation.3 | async-start | bytes 4423680
  29.7 15.3 %copy-start.3 = (bf16[1,2560]{1,0:T(2,128)(2,1)S(1)}, bf16[1,2560]{1,0:T(2,128)(2,1)}, u32[]{:S(2)}) copy-start(bf16[1,2560]{1,0:T(2,128)(2,1)} %param.16) | copy-start | bytes 15364
  29.7 15.3 %copy-start.1 = (bf16[1,90,2560]{2,1,0:T(8,128)(2,1)S(1)}, bf16[1,90,2560]{2,1,0:T(8,128)(2,1)}, u32[]{:S(2)}) copy-start(bf16[1,90,2560]{2,1,0:T(8,128)(2,1)} %param.15) | copy-start | bytes 1382404
  314.1 8.9 %copy-start.4 = (bf16[1,1440]{1,0:T(2,128)(2,1)S(1)}, bf16[1,1440]{1,0:T(2,128)(2,1)}, u32[]{:S(2)}) copy-start(bf16[1,1440]{1,0:T(2,128)(2,1)} %param.19) | copy-start | bytes 8644
  323.1 55.2 %copy-start.5 = (f32[64,4]{0,1:T(4,128)S(1)}, f32[64,4]{0,1:T(4,128)}, u32[]{:S(2)}) copy-start(f32[64,4]{0,1:T(4,128)} %param.12) | copy-start | bytes 3076
  323.1 92.9 %copy-start = (bf16[64,2880]{1,0:T(8,128)(2,1)S(1)}, bf16[64,2880]{1,0:T(8,128)(2,1)}, u32[]{:S(2)}) copy-start(bf16[64,2880]{1,0:T(8,128)(2,1)} %param.10) | copy-start | bytes 1105924
  373.6 42.4 %all-to-all-start.1 = ((bf16[8,64,1440]{2,1,0:T(8,128)(2,1)}), bf16[8,64,1440]{2,1,0:T(8,128)(2,1)S(1)}, u32[]{:S(2)}, u32[]{:S(2)}) async-start(bf16[8,64,1440]{2,1,0:T(8,128)(2,1)} %add_convert_fusion), calls=%async_computation.1 | async-start | bytes 3145728 | tf_op jit(solution)/shard_map/all_to_all | solution.py:100
Sparse Core Ops, SparseCore 0:
  323.2 40.1 reduce-scatter.3
where the time goes:
time: 426 us; the launch traced here: 424 us
  local copies, waits for them, and re-layouts  242 us (57%)
  waiting for transfers between devices  98.3 us (23%)
  matrix products  33.6 us (8%)
  other arithmetic  26.2 us (6%)
  between operations  13.6 us (3%)
  starting transfers between devices  11.2 us (3%)
    slice x1, local copies, waits for them, and re-layouts, shards(): upward = jnp.clip(projected[:, 1::2], -7.0, 7.0)  91.9 us
    slice x1, local copies, waits for them, and re-layouts, shards(): gate_part = jnp.minimum(projected[:, 0::2], 7.0)  91.5 us
    unnamed x2, waiting for transfers between devices  40.3 us
    all_to_all x1, waiting for transfers between devices, shards(): lax.all_to_all(answered, 'ep', split_axis=0, concat_axis=0, tiled=True)  37.7 us
    unnamed x17, local copies, waits for them, and re-layouts  23 us
    mul x2, local copies, waits for them, and re-layouts, unpack_weights(): signed_val.reshape(row_count // 32, 32, -1)  21.6 us
    all_to_all x1, waiting for transfers between devices, shards(): lax.all_to_all(outgoing, 'ep', split_axis=0, concat_axis=0, tiled=True)  20.4 us
    convert_element_type x1, other arithmetic, unpack_rows(): return signed_val.reshape(row_count, -1).astype(jnp.bfloat16)  19.6 us
  transfers between devices with their start and end apart: 3, of which 3 were waited for; matrix products, arithmetic and copies ran while one was open for 11% of the time, Pallas kernels for 0%

commit v1 on v0

v1 whole, which is shorter than its diff:
```python
import jax
import jax.numpy as jnp
from jax import lax
from jax.experimental import pallas as pl
from jax.experimental.pallas import tpu as pltpu
from jax.sharding import PartitionSpec as P

VMEM_BYTES = 56 * 1024 * 1024


def largest_step(total, limit, multiple):
    best = 0
    for size in range(multiple, min(total, limit) + 1, multiple):
        if total % size == 0:
            best = size
    return best or total


def decode_words(words, scale):
    word_count, width = words.shape
    shifts = lax.broadcasted_iota(jnp.int32, (1, 8, width), 1) * 4
    nibble = (words[:, None, :] >> shifts) & 15
    half = nibble.astype(jnp.float32).reshape(word_count * 8, width).astype(jnp.bfloat16) * 0.5
    negative = half >= 4.0
    magnit = jnp.where(negative, half - 4.0, half)
    value = magnit + jnp.maximum(magnit - 2.0, 0.0) + 2.0 * jnp.maximum(magnit - 3.0, 0.0)
    return value * jnp.where(negative, -scale, scale)


def gate_up_kernel(words_ref, scale_ref, out_ref, *, step, block_words):
    width = words_ref.shape[1]
    half = width // 2
    from_col = lax.broadcasted_iota(jnp.int32, (width, width), 0)
    to_col = lax.broadcasted_iota(jnp.int32, (width, width), 1)
    wanted = jnp.where(to_col < half, 2 * to_col, 2 * (to_col - half) + 1)
    parting = (from_col == wanted).astype(jnp.bfloat16)
    blocks = step // block_words
    scales = scale_ref[...].astype(jnp.float32)
    for part in range(words_ref.shape[0] // step):
        words = words_ref[part * step : (part + 1) * step, :]
        scale = scales[part * blocks : (part + 1) * blocks, :]
        spread = jnp.broadcast_to(scale[:, None, :], (blocks, block_words * 8, width))
        spread = spread.reshape(step * 8, width).astype(jnp.bfloat16)
        value = decode_words(words, spread)
        out_ref[part * step * 8 : (part + 1) * step * 8, :] = jnp.dot(
            value, parting, preferred_element_type=jnp.float32
        ).astype(jnp.bfloat16)


def unpack_gate_up(codes, scales, tile):
    word_count, width = codes.shape
    block_words = word_count // scales.shape[0]
    step = largest_step(word_count, 80, 8)
    return pl.pallas_call(
        lambda *refs: gate_up_kernel(*refs, step=step, block_words=block_words),
        grid=(width // tile,),
        in_specs=[
            pl.BlockSpec((word_count, tile), lambda i: (0, i)),
            pl.BlockSpec((scales.shape[0], tile), lambda i: (0, i)),
        ],
        out_specs=pl.BlockSpec((word_count * 8, tile), lambda i: (0, i)),
        out_shape=jax.ShapeDtypeStruct((word_count * 8, width), jnp.bfloat16),
        compiler_params=pltpu.CompilerParams(vmem_limit_bytes=VMEM_BYTES),
        name="unpack_gate_up",
    )(codes, scales)


def down_kernel(words_ref, scale_ref, out_ref):
    unit_count = words_ref.shape[1]
    block_count = scale_ref.shape[1]
    width = unit_count // block_count
    block_of = lax.broadcasted_iota(jnp.int32, (block_count, unit_count), 1) // width
    spreading = (block_of == lax.broadcasted_iota(jnp.int32, (block_count, unit_count), 0)).astype(
        jnp.bfloat16
    )
    spread = jnp.dot(scale_ref[...], spreading, preferred_element_type=jnp.float32)
    out_ref[...] = decode_words(words_ref[...], spread.astype(jnp.bfloat16))


def unpack_down(codes, scales):
    unit_count, word_count = codes.shape
    block_count = scales.shape[0]
    step = largest_step(word_count, 40, 8)
    return pl.pallas_call(
        down_kernel,
        grid=(word_count // step,),
        in_specs=[
            pl.BlockSpec((step, unit_count), lambda i: (i, 0)),
            pl.BlockSpec((step * 8, block_count), lambda i: (i, 0)),
        ],
        out_specs=pl.BlockSpec((step * 8, unit_count), lambda i: (i, 0)),
        out_shape=jax.ShapeDtypeStruct((word_count * 8, unit_count), jnp.bfloat16),
        compiler_params=pltpu.CompilerParams(vmem_limit_bytes=VMEM_BYTES),
        name="unpack_down",
    )(codes.T, scales.T)


def hidden_kernel(rows_ref, weight_ref, bias_ref, out_ref):
    model_width, width = weight_ref.shape
    half = width // 2
    projected = jnp.dot(
        rows_ref[:, :model_width], weight_ref[...], preferred_element_type=jnp.float32
    ) + bias_ref[...]
    gate = jnp.minimum(projected[:, :half], 7.0)
    upward = jnp.clip(projected[:, half:], -7.0, 7.0)
    out_ref[...] = (gate * jax.nn.sigmoid(1.702 * gate) * (upward + 1.0)).astype(jnp.bfloat16)


def hidden_units(rows, weight, bias, tile):
    row_count = rows.shape[0]
    model_width, width = weight.shape
    return pl.pallas_call(
        hidden_kernel,
        grid=(width // tile,),
        in_specs=[
            pl.BlockSpec(rows.shape, lambda i: (0, 0)),
            pl.BlockSpec((model_width, tile), lambda i: (0, i)),
            pl.BlockSpec((1, tile), lambda i: (0, i)),
        ],
        out_specs=pl.BlockSpec((row_count, tile // 2), lambda i: (0, i)),
        out_shape=jax.ShapeDtypeStruct((row_count, width // 2), jnp.bfloat16),
        compiler_params=pltpu.CompilerParams(vmem_limit_bytes=VMEM_BYTES),
        name="hidden_units",
    )(rows, weight, bias)


def project_kernel(rows_ref, weight_ref, bias_ref, factor_ref, out_ref):
    value = lax.dot_general(
        rows_ref[...], weight_ref[...], (((1,), (1,)), ((), ())), preferred_element_type=jnp.float32
    )
    out_ref[...] = ((value + bias_ref[...]) * factor_ref[...]).astype(jnp.bfloat16)


def project_down(rows, weight, bias, factor):
    row_count, unit_count = rows.shape
    model_width = weight.shape[0]
    tile = 512
    return pl.pallas_call(
        project_kernel,
        grid=(pl.cdiv(model_width, tile),),
        in_specs=[
            pl.BlockSpec((row_count, unit_count), lambda i: (0, 0)),
            pl.BlockSpec((tile, unit_count), lambda i: (i, 0)),
            pl.BlockSpec((1, tile), lambda i: (0, i)),
            pl.BlockSpec((row_count, 1), lambda i: (0, 0)),
        ],
        out_specs=pl.BlockSpec((row_count, tile), lambda i: (0, i)),
        out_shape=jax.ShapeDtypeStruct((row_count, model_width), jnp.bfloat16),
        compiler_params=pltpu.CompilerParams(vmem_limit_bytes=VMEM_BYTES),
        name="project_down",
    )(rows, weight, bias, factor)


def rms_normed(hidden, norm_gain):
    widened = hidden.astype(jnp.float32)
    mean_square = jnp.mean(widened * widened, axis=-1, keepdims=True)
    scaled = widened * lax.rsqrt(mean_square + 1e-05) * norm_gain.astype(jnp.float32)
    return scaled.astype(jnp.bfloat16)


def parted_bias(bias, tile):
    width = bias.shape[1]
    return bias.reshape(width // tile, tile // 2, 2).swapaxes(1, 2).reshape(1, width).astype(jnp.float32)


def shards(
    hidden,
    route_experts,
    route_weight,
    norm_gain,
    gate_up_codes,
    gate_up_scales,
    gate_up_bias,
    down_codes,
    down_scales,
    down_bias,
):
    ep_count = lax.axis_size("ep")
    ep_rank = lax.axis_index("ep")
    tp_count = lax.axis_size("tp")
    tp_rank = lax.axis_index("tp")
    tok_count, model_width = hidden.shape
    top_count = route_experts.shape[1]
    quarter = model_width // tp_count
    tile = 256
    capacity = min(tok_count, max(tp_count, 2 * tok_count * top_count // ep_count))
    normed = rms_normed(hidden, norm_gain)
    gate_up_weight = unpack_gate_up(gate_up_codes[0], gate_up_scales[0], tile)
    down_weight = unpack_down(down_codes[0], down_scales[0])
    up_bias = parted_bias(gate_up_bias, tile)
    own_cols = lax.dynamic_slice_in_dim(hidden, tp_rank * quarter, quarter, 1).astype(jnp.float32)
    own_bias = down_bias.astype(jnp.float32)
    lower_bias = lax.dynamic_update_slice(
        jnp.zeros((1, model_width), jnp.float32), own_bias, (0, tp_rank * quarter)
    )

    if capacity == tok_count:
        experts = jnp.arange(ep_count, dtype=jnp.int32)
        factors = jnp.sum(
            jnp.where(route_experts[:, :, None] == experts, route_weight[:, :, None], 0.0), axis=1
        )
        upper = factors.astype(jnp.bfloat16)
        rest = factors - upper.astype(jnp.float32)
        middle = rest.astype(jnp.bfloat16)
        lowest = (rest - middle.astype(jnp.float32)).astype(jnp.bfloat16)
        outgoing = jnp.concatenate([normed, upper, middle, lowest], axis=1)
        arrived = lax.all_gather(outgoing, "ep", axis=0, tiled=True)
        tail = arrived[:, model_width:].astype(jnp.float32)
        split = tail.reshape(tail.shape[0], 3, ep_count)
        factor = jnp.sum(
            jnp.where(experts == ep_rank, split, 0.0), axis=(1, 2)
        ).reshape(-1, 1)
        activated = hidden_units(arrived, gate_up_weight, up_bias, tile)
        answered = project_down(activated, down_weight, lower_bias, factor)
        summed = lax.psum_scatter(answered, "ep", scatter_dimension=0, tiled=True)
        summed = lax.psum_scatter(summed, "tp", scatter_dimension=1, tiled=True)
        return (own_cols + summed.astype(jnp.float32)).astype(jnp.bfloat16)

    flat_routes = route_experts.reshape(-1)
    onehot = (flat_routes[:, None] == jnp.arange(ep_count, dtype=jnp.int32)[None, :]).astype(
        jnp.int32
    )
    before = jnp.cumsum(onehot, axis=0) - onehot
    slot_of = jnp.sum(before * onehot, axis=1)
    target = (flat_routes * capacity + slot_of).reshape(tok_count, top_count)
    columns = jnp.arange(ep_count * capacity, dtype=jnp.int32)
    matches = target[:, :, None] == columns[None, None, :]
    placing = jnp.any(matches, axis=1).astype(jnp.bfloat16)
    weighting = jnp.sum(jnp.where(matches, route_weight[:, :, None], 0.0), axis=1)
    outgoing = lax.dot_general(
        placing, normed, (((0,), (0,)), ((), ())), preferred_element_type=jnp.float32
    ).astype(jnp.bfloat16)
    outgoing = outgoing.reshape(ep_count, capacity, model_width)
    arrived = lax.all_to_all(outgoing, "ep", split_axis=0, concat_axis=0, tiled=True)
    flat_rows = arrived.reshape(ep_count * capacity, model_width)
    activated = hidden_units(flat_rows, gate_up_weight, up_bias, tile)
    ones = jnp.ones((ep_count * capacity, 1), jnp.float32)
    partial_value = project_down(activated, down_weight, lower_bias, ones)
    answered = lax.psum_scatter(partial_value, "tp", scatter_dimension=1, tiled=True)
    answered = answered.reshape(ep_count, capacity, quarter)
    came_back = lax.all_to_all(answered, "ep", split_axis=0, concat_axis=0, tiled=True)
    gathered = came_back.reshape(ep_count * capacity, quarter).astype(jnp.float32)
    layer_out = own_cols + jnp.dot(weighting, gathered, precision=lax.Precision.HIGHEST)
    return layer_out.astype(jnp.bfloat16)


def solution(mesh):
    placed = (
        P(("groups", "ep"), None),
        P(("groups", "ep"), None),
        P(("groups", "ep"), None),
        P(),
        P("ep", None, "tp"),
        P("ep", None, "tp"),
        P("ep", "tp"),
        P("ep", "tp", None),
        P("ep", "tp", None),
        P("ep", "tp"),
    )
    return jax.shard_map(
        shards, mesh=mesh, in_specs=placed, out_specs=P(("groups", "ep"), "tp"), check_vma=False
    )
```

time: 426 us -> 145 us (0.34)
  local copies, waits for them, and re-layouts: 242 us -> 8.35 us
  Pallas kernels: 0 us -> 53.1 us
  waiting for transfers between devices: 98.3 us -> 62.5 us
  matrix products: 33.6 us -> 0 us
  other arithmetic: 26.2 us -> 6.45 us
  starting transfers between devices: 11.2 us -> 0.09 us
    slice x3 -> x0, local copies, waits for them, and re-layouts: 184 us -> none  [the longest x1 91.9 us: shards(): upward = jnp.clip(projected[:, 1::2], -7.0, 7.0)]
    all_to_all x2 -> x0, waiting for transfers between devices: 58 us -> none  [the longest x1 37.7 us: shards(): lax.all_to_all(answered, 'ep', split_axis=0, concat_axis=0, tiled=True)]
    pallas_call x0 -> x4, Pallas kernels: none -> 53.1 us  [the longest x1 17.6 us: unpack_gate_up(): pl.pallas_call(lambda *refs: gate_up_kernel(*refs, step=step, block_words...]
    reduce_scatter x0 -> x1, waiting for transfers between devices: none -> 38.4 us  [shards(): summed = lax.psum_scatter(answered, 'ep', scatter_dimension=0, tiled=True)]
    dot_general x4 -> x0, matrix products: 33.6 us -> none  [the longest x1 16.8 us: shards(): jnp.dot(activated, down_weight, preferred_element_type=jnp.float32)]
    unnamed x2 -> x4, waiting for transfers between devices: 40.3 us -> 16.8 us
    mul x2 -> x0, local copies, waits for them, and re-layouts: 21.6 us -> none  [unpack_weights(): signed_val.reshape(row_count // 32, 32, -1)]
    convert_element_type x6, other arithmetic: 22.6 us -> 2.72 us  [the longest x1 1.16 us: rms_normed(): return scaled.astype(jnp.bfloat16)]
  transfers between devices with their start and end apart: 3 -> 3, of which waited for: 3 -> 3; matrix products, arithmetic and copies ran while one was open for 11% -> 3% of each run, Pallas kernels for 0% -> 20%
where the time goes in v1:
time: 145 us; the launch traced here: 144 us
  waiting for transfers between devices  62.5 us (43%)
  Pallas kernels  53.1 us (37%)
  between operations  13.2 us (9%)
  local copies, waits for them, and re-layouts  8.35 us (6%)
  other arithmetic  6.45 us (4%)
    reduce_scatter x1, waiting for transfers between devices, shards(): summed = lax.psum_scatter(answered, 'ep', scatter_dimension=0, tiled=True)  38.4 us
    pallas_call x1, Pallas kernels, unpack_gate_up(): pl.pallas_call(lambda *refs: gate_up_kernel(*refs, step=step, block_words...  17.6 us
    unnamed x4, waiting for transfers between devices  16.8 us
    pallas_call x1, Pallas kernels, hidden_units(): pl.pallas_call(hidden_kernel, grid=(width // tile,), in_specs=[pl.BlockSp...  15 us
    pallas_call x1, Pallas kernels, unpack_down(): pl.pallas_call(down_kernel, grid=(word_count // step,), in_specs=[pl.Bloc...  11.2 us
    pallas_call x1, Pallas kernels, project_down(): pl.pallas_call(project_kernel, grid=(pl.cdiv(model_width, tile),), in_spe...  9.28 us
    all_gather x1, waiting for transfers between devices, shards(): arrived = lax.all_gather(outgoing, 'ep', axis=0, tiled=True)  7.29 us
    unnamed x11, local copies, waits for them, and re-layouts  4.51 us
  transfers between devices with their start and end apart: 3, of which 3 were waited for; matrix products, arithmetic and copies ran while one was open for 3% of the time, Pallas kernels for 20%

profile of v1, /device:TPU:0, one launch (start us, length us, event | category | flops | bytes accessed | tf_op | source)
XLA Modules:
  0.0 143.6 jit_solution(2170940215755241764)
XLA Ops:
  6.5 0.0 copy-start.1
  6.5 0.0 copy-start.3
  6.5 0.0 all-gather.2.cloned.1.call-start
  6.5 0.7 select_reduce_fusion.1
  7.3 0.1 copy.30
  7.4 0.1 copy.32
  7.5 0.1 copy.31
  7.6 0.7 convert_element_type.50
  8.3 1.2 fusion
  9.4 1.2 fusion.2
  10.6 0.9 concatenate.3
  11.5 0.0 all-gather.2.cloned.1.call-update
  11.5 0.0 reduce-scatter.5.cloned.1.call-start
  11.6 0.7 convert_reduce_fusion
  12.3 0.6 reshape.36
  12.9 0.8 copy.33
  13.8 0.0 copy-done.1
  13.8 1.2 copy.34
  15.0 0.0 copy-done.3
  15.0 0.1 broadcast_in_dim.36
  15.1 17.6 %unpack_gate_up.1.weight_ref = bf16[2880,2560]{1,0:T(8,128)(2,1)} custom-call(s32[360,2560]{1,0:T(8,128)} %bitcast.13, bf16[90,2560]{1,0:T(8,128)(2,1)} %bitcast.18), custom_call_target="tpu_custom_call" | custom-call | tf_op jit(solution)/shard_map/unpack_gate_up/pallas_call | solution.py:54
  32.7 11.2 %unpack_down.1.weight_ref = bf16[2880,1280]{1,0:T(8,128)(2,1)} custom-call(s32[360,1280]{1,0:T(8,128)} %bitcast.17, bf16[2880,40]{1,0:T(8,128)(2,1)} %bitcast.14), custom_call_target="tpu_custom_call" | custom-call | tf_op jit(solution)/shard_map/unpack_down/pallas_call | solution.py:84
  43.9 0.3 dynamic_update_slice.3.bias_ref
  44.2 0.0 copy-start.2
  44.2 7.3 %all-gather.2.cloned.1.call-done.rows_ref = bf16[512,2904]{1,0:T(8,128)(2,1)} async-done(((bf16[64,2904]{1,0:T(8,128)(2,1)}), bf16[512,2904]{1,0:T(8,128)(2,1)}) %all-gather.2.cloned.1.call-update) | async-done | bytes 2973712 | tf_op jit(solution)/shard_map/all_gather | solution.py:207
  51.5 1.1 select_reduce_fusion
  52.6 0.9 copy.35.factor_ref
  53.5 15.0 %hidden_units.1.rows_ref = bf16[512,1280]{1,0:T(8,128)(2,1)} custom-call(bf16[512,2904]{1,0:T(8,128)(2,1)} %all-gather.2.cloned.1.call-done.rows_ref, bf16[2880,2560]{1,0:T(8,128)(2,1)} %unpack_gate_up.1.weight_ref, f32[1,2560]{1,0:T(1,128)} %bitcast.20), custom_call_target="tpu_custom_call" | custom-call | tf_op jit(solution)/shard_map/hidden_units/pallas_call | solution.py:112
  68.5 0.0 copy-done.2
  68.5 9.3 %project_down.1 = bf16[512,2880]{1,0:T(8,128)(2,1)} custom-call(bf16[512,1280]{1,0:T(8,128)(2,1)} %hidden_units.1.rows_ref, bf16[2880,1280]{1,0:T(8,128)(2,1)} %unpack_down.1.weight_ref, f32[1,2880]{1,0:T(1,128)} %copy-done.2, f32[512,1]{1,0:T(8,128)} %copy.35.factor_ref), custom_call_target="tpu_custom_call" | custom-call | tf_op jit(solution)/shard_map/project_down/pallas_call | solution.py:138
  77.8 0.0 copy-start
  77.8 0.0 reduce-scatter.5.cloned.1.call-update
  77.8 0.0 reduce-scatter.7.cloned.1.call-start
  77.8 38.4 %reduce-scatter.5.cloned.1.call-done = bf16[64,2880]{1,0:T(8,128)(2,1)} async-done(((bf16[512,2880]{1,0:T(8,128)(2,1)}), bf16[64,2880]{1,0:T(8,128)(2,1)}) %reduce-scatter.5.cloned.1.call-update) | async-done | bytes 368656 | tf_op jit(solution)/shard_map/reduce_scatter | solution.py:215
  116.2 2.1 %copy.36 = bf16[64,2880]{0,1:T(8,128)(2,1)} copy(bf16[64,2880]{1,0:T(8,128)(2,1)} %reduce-scatter.5.cloned.1.call-done) | data formatting | bytes 737280
  118.3 0.0 reduce-scatter.7.cloned.1.call-update
  118.4 16.8 %reduce-scatter.7.cloned.1.call-done = bf16[1440,64]{1,0:T(8,128)(2,1)} async-done(((bf16[2880,64]{1,0:T(8,128)(2,1)}), bf16[1440,64]{1,0:T(8,128)(2,1)}) %reduce-scatter.7.cloned.1.call-update) | async-done | bytes 184336
  135.1 1.1 copy.37
  136.3 0.0 copy-done
  136.3 0.8 add_convert_fusion
  (7 shorter events, 0.0 us)
Async XLA Ops:
  6.5 7.2 %copy-start.1 = (bf16[1,40,2880]{2,1,0:T(8,128)(2,1)S(1)}, bf16[1,40,2880]{2,1,0:T(8,128)(2,1)}, u32[]{:S(2)}) copy-start(bf16[1,40,2880]{2,1,0:T(8,128)(2,1)} %param.18) | copy-start | bytes 691204
  6.5 8.4 %copy-start.3 = (bf16[1,1440]{1,0:T(2,128)(2,1)S(1)}, bf16[1,1440]{1,0:T(2,128)(2,1)}, u32[]{:S(2)}) copy-start(bf16[1,1440]{1,0:T(2,128)(2,1)} %param.19) | copy-start | bytes 8644
  6.5 44.9 %all-gather.2.cloned.1.call-start = ((), (), s32[]{:S(2)}) async-start(), calls=%async_computation.2 | async-start | bytes 3391488 | tf_op jit(solution)/shard_map/all_gather | solution.py:207
  11.5 104.7 %reduce-scatter.5.cloned.1.call-start = ((), (), s32[]{:S(2)}) async-start(), calls=%async_computation.3 | async-start | bytes 3391488 | tf_op jit(solution)/shard_map/reduce_scatter | solution.py:215
  44.2 24.3 %copy-start.2 = (f32[1,2880]{1,0:T(1,128)}, f32[1,2880]{1,0:T(1,128)S(1)}, u32[]{:S(2)}) copy-start(f32[1,2880]{1,0:T(1,128)S(1)} %dynamic_update_slice.3.bias_ref) | copy-start | bytes 34564
  77.8 58.5 %copy-start = (bf16[64,2880]{1,0:T(8,128)(2,1)S(1)}, bf16[64,2880]{1,0:T(8,128)(2,1)}, u32[]{:S(2)}) copy-start(bf16[64,2880]{1,0:T(8,128)(2,1)} %param.10) | copy-start | bytes 1105924
  77.8 57.3 %reduce-scatter.7.cloned.1.call-start = ((), (), s32[]{:S(2)}) async-start(), calls=%async_computation.4 | async-start | bytes 1105920
Sparse Core Ops, SparseCore 0:
  11.6 39.7 all-gather.1
  77.9 38.2 reduce-scatter.4
  118.5 16.5 reduce-scatter.6

commit v2 on v1

--- a/solution.py
+++ b/solution.py
@@ -6,6 +6,7 @@
 from jax.sharding import PartitionSpec as P
 
 VMEM_BYTES = 56 * 1024 * 1024
+PIECES = 2
 
 
 def largest_step(total, limit, multiple):
@@ -27,13 +28,14 @@
     return value * jnp.where(negative, -scale, scale)
 
 
-def gate_up_kernel(words_ref, scale_ref, out_ref, *, step, block_words):
+def gate_up_kernel(words_ref, scale_ref, bias_ref, out_ref, bias_out_ref, *, step, block_words):
     width = words_ref.shape[1]
     half = width // 2
     from_col = lax.broadcasted_iota(jnp.int32, (width, width), 0)
     to_col = lax.broadcasted_iota(jnp.int32, (width, width), 1)
     wanted = jnp.where(to_col < half, 2 * to_col, 2 * (to_col - half) + 1)
     parting = (from_col == wanted).astype(jnp.bfloat16)
+    bias_out_ref[...] = jnp.dot(bias_ref[...], parting, preferred_element_type=jnp.float32)
     blocks = step // block_words
     scales = scale_ref[...].astype(jnp.float32)
     for part in range(words_ref.shape[0] // step):
@@ -47,7 +49,7 @@
         ).astype(jnp.bfloat16)
 
 
-def unpack_gate_up(codes, scales, tile):
+def unpack_gate_up(codes, scales, bias, tile):
     word_count, width = codes.shape
     block_words = word_count // scales.shape[0]
     step = largest_step(word_count, 80, 8)
@@ -57,12 +59,19 @@
         in_specs=[
             pl.BlockSpec((word_count, tile), lambda i: (0, i)),
             pl.BlockSpec((scales.shape[0], tile), lambda i: (0, i)),
-        ],
-        out_specs=pl.BlockSpec((word_count * 8, tile), lambda i: (0, i)),
-        out_shape=jax.ShapeDtypeStruct((word_count * 8, width), jnp.bfloat16),
+            pl.BlockSpec((1, tile), lambda i: (0, i)),
+        ],
+        out_specs=[
+            pl.BlockSpec((word_count * 8, tile), lambda i: (0, i)),
+            pl.BlockSpec((1, tile), lambda i: (0, i)),
+        ],
+        out_shape=[
+            jax.ShapeDtypeStruct((word_count * 8, width), jnp.bfloat16),
+            jax.ShapeDtypeStruct((1, width), jnp.float32),
+        ],
         compiler_params=pltpu.CompilerParams(vmem_limit_bytes=VMEM_BYTES),
         name="unpack_gate_up",
-    )(codes, scales)
+    )(codes, scales, bias)
 
 
 def down_kernel(words_ref, scale_ref, out_ref):
@@ -124,14 +133,15 @@
     )(rows, weight, bias)
 
 
-def project_kernel(rows_ref, weight_ref, bias_ref, factor_ref, out_ref):
+def project_kernel(rows_ref, weight_ref, bias_ref, tail_ref, pick_ref, out_ref):
     value = lax.dot_general(
         rows_ref[...], weight_ref[...], (((1,), (1,)), ((), ())), preferred_element_type=jnp.float32
     )
-    out_ref[...] = ((value + bias_ref[...]) * factor_ref[...]).astype(jnp.bfloat16)
-
-
-def project_down(rows, weight, bias, factor):
+    factor = jnp.sum(tail_ref[...].astype(jnp.float32) * pick_ref[...], axis=1, keepdims=True)
+    out_ref[...] = ((value + bias_ref[...]) * factor).astype(jnp.bfloat16)
+
+
+def project_down(rows, weight, bias, tail, pick):
     row_count, unit_count = rows.shape
     model_width = weight.shape[0]
     tile = 512
@@ -142,13 +152,52 @@
             pl.BlockSpec((row_count, unit_count), lambda i: (0, 0)),
             pl.BlockSpec((tile, unit_count), lambda i: (i, 0)),
             pl.BlockSpec((1, tile), lambda i: (0, i)),
-            pl.BlockSpec((row_count, 1), lambda i: (0, 0)),
+            pl.BlockSpec((row_count, 128), lambda i: (0, tail.shape[1] // 128 - 1)),
+            pl.BlockSpec((1, 128), lambda i: (0, 0)),
         ],
         out_specs=pl.BlockSpec((row_count, tile), lambda i: (0, i)),
         out_shape=jax.ShapeDtypeStruct((row_count, model_width), jnp.bfloat16),
         compiler_params=pltpu.CompilerParams(vmem_limit_bytes=VMEM_BYTES),
         name="project_down",
-    )(rows, weight, bias, factor)
+    )(rows, weight, bias, tail, pick)
+
+
+def norm_kernel(hidden_ref, gain_ref, experts_ref, weight_ref, *out_refs, ep_count):
+    tok_count, model_width = hidden_ref.shape
+    total = out_refs[0].shape[1]
+    widened = hidden_ref[...].astype(jnp.float32)
+    mean_square = jnp.mean(widened * widened, axis=-1, keepdims=True)
+    normed = (widened * lax.rsqrt(mean_square + 1e-05) * gain_ref[...].astype(jnp.float32)).astype(
+        jnp.bfloat16
+    )
+    tail = total - model_width
+    place = lax.broadcasted_iota(jnp.int32, (tok_count, tail), 1) - (tail - 3 * ep_count)
+    factor = jnp.zeros((tok_count, tail), jnp.float32)
+    for position in range(experts_ref.shape[1]):
+        chosen = experts_ref[:, position : position + 1]
+        named = (place == chosen) | (place == chosen + ep_count) | (place == chosen + 2 * ep_count)
+        factor = factor + jnp.where(named, weight_ref[:, position : position + 1], 0.0)
+    upper = factor.astype(jnp.bfloat16).astype(jnp.float32)
+    rest = factor - upper
+    middle = rest.astype(jnp.bfloat16).astype(jnp.float32)
+    pieces = jnp.where(place < ep_count, upper, jnp.where(place < 2 * ep_count, middle, rest - middle))
+    pieces = pieces.astype(jnp.bfloat16)
+    step = tok_count // len(out_refs)
+    for i, out_ref in enumerate(out_refs):
+        out_ref[:, :model_width] = normed[i * step : (i + 1) * step]
+        out_ref[:, model_width:] = pieces[i * step : (i + 1) * step]
+
+
+def normed_with_factors(hidden, gain, route_experts, route_weight, ep_count, pieces):
+    tok_count, model_width = hidden.shape
+    total = -(-(model_width + 3 * ep_count) // 128) * 128
+    shape = jax.ShapeDtypeStruct((tok_count // pieces, total), jnp.bfloat16)
+    return pl.pallas_call(
+        lambda *refs: norm_kernel(*refs, ep_count=ep_count),
+        out_shape=[shape] * pieces,
+        compiler_params=pltpu.CompilerParams(vmem_limit_bytes=VMEM_BYTES),
+        name="norm",
+    )(hidden, gain.reshape(1, -1), route_experts, route_weight)
 
 
 def rms_normed(hidden, norm_gain):
@@ -158,9 +207,14 @@
     return scaled.astype(jnp.bfloat16)
 
 
-def parted_bias(bias, tile):
-    width = bias.shape[1]
-    return bias.reshape(width // tile, tile // 2, 2).swapaxes(1, 2).reshape(1, width).astype(jnp.float32)
+def tp_sum(rows, tp_rank, tp_count, quarter):
+    summed = lax.dynamic_slice_in_dim(rows, tp_rank * quarter, quarter, 1).astype(jnp.float32)
+    for away in range(1, tp_count):
+        other = (tp_rank + away) % tp_count
+        sent = lax.dynamic_slice_in_dim(rows, other * quarter, quarter, 1)
+        got = lax.ppermute(sent, "tp", [(k, (k + away) % tp_count) for k in range(tp_count)])
+        summed = summed + got.astype(jnp.float32)
+    return summed
 
 
 def shards(
@@ -184,38 +238,33 @@
     quarter = model_width // tp_count
     tile = 256
     capacity = min(tok_count, max(tp_count, 2 * tok_count * top_count // ep_count))
-    normed = rms_normed(hidden, norm_gain)
-    gate_up_weight = unpack_gate_up(gate_up_codes[0], gate_up_scales[0], tile)
+    gate_up_weight, up_bias = unpack_gate_up(
+        gate_up_codes[0], gate_up_scales[0], gate_up_bias, tile
+    )
     down_weight = unpack_down(down_codes[0], down_scales[0])
-    up_bias = parted_bias(gate_up_bias, tile)
     own_cols = lax.dynamic_slice_in_dim(hidden, tp_rank * quarter, quarter, 1).astype(jnp.float32)
     own_bias = down_bias.astype(jnp.float32)
     lower_bias = lax.dynamic_update_slice(
         jnp.zeros((1, model_width), jnp.float32), own_bias, (0, tp_rank * quarter)
     )
 
-    if capacity == tok_count:
-        experts = jnp.arange(ep_count, dtype=jnp.int32)
-        factors = jnp.sum(
-            jnp.where(route_experts[:, :, None] == experts, route_weight[:, :, None], 0.0), axis=1
+    if capacity == tok_count and 3 * ep_count <= 128:
+        place = jnp.arange(128, dtype=jnp.int32) - (128 - 3 * ep_count)
+        pick = ((place >= 0) & (place % ep_count == ep_rank)).astype(jnp.float32).reshape(1, 128)
+        outgoing = normed_with_factors(
+            hidden, norm_gain, route_experts, route_weight, ep_count, PIECES
         )
-        upper = factors.astype(jnp.bfloat16)
-        rest = factors - upper.astype(jnp.float32)
-        middle = rest.astype(jnp.bfloat16)
-        lowest = (rest - middle.astype(jnp.float32)).astype(jnp.bfloat16)
-        outgoing = jnp.concatenate([normed, upper, middle, lowest], axis=1)
-        arrived = lax.all_gather(outgoing, "ep", axis=0, tiled=True)
-        tail = arrived[:, model_width:].astype(jnp.float32)
-        split = tail.reshape(tail.shape[0], 3, ep_count)
-        factor = jnp.sum(
-            jnp.where(experts == ep_rank, split, 0.0), axis=(1, 2)
-        ).reshape(-1, 1)
-        activated = hidden_units(arrived, gate_up_weight, up_bias, tile)
-        answered = project_down(activated, down_weight, lower_bias, factor)
-        summed = lax.psum_scatter(answered, "ep", scatter_dimension=0, tiled=True)
-        summed = lax.psum_scatter(summed, "tp", scatter_dimension=1, tiled=True)
-        return (own_cols + summed.astype(jnp.float32)).astype(jnp.bfloat16)
-
+        arrived = [lax.all_gather(rows, "ep", axis=0, tiled=True) for rows in outgoing]
+        outputs = []
+        for rows in arrived:
+            activated = hidden_units(rows, gate_up_weight, up_bias, tile)
+            answered = project_down(activated, down_weight, lower_bias, rows, pick)
+            summed = lax.psum_scatter(answered, "ep", scatter_dimension=0, tiled=True)
+            outputs.append(tp_sum(summed, tp_rank, tp_count, quarter))
+        summed = jnp.concatenate(outputs, axis=0)
+        return (own_cols + summed).astype(jnp.bfloat16)
+
+    normed = rms_normed(hidden, norm_gain)
     flat_routes = route_experts.reshape(-1)
     onehot = (flat_routes[:, None] == jnp.arange(ep_count, dtype=jnp.int32)[None, :]).astype(
         jnp.int32
@@ -234,8 +283,10 @@
     arrived = lax.all_to_all(outgoing, "ep", split_axis=0, concat_axis=0, tiled=True)
     flat_rows = arrived.reshape(ep_count * capacity, model_width)
     activated = hidden_units(flat_rows, gate_up_weight, up_bias, tile)
-    ones = jnp.ones((ep_count * capacity, 1), jnp.float32)
-    partial_value = project_down(activated, down_weight, lower_bias, ones)
+    ones = jnp.full((ep_count * capacity, 128), 1.0 / 128, jnp.bfloat16)
+    partial_value = project_down(
+        activated, down_weight, lower_bias, ones, jnp.ones((1, 128), jnp.float32)
+    )
     answered = lax.psum_scatter(partial_value, "tp", scatter_dimension=1, tiled=True)
     answered = answered.reshape(ep_count, capacity, quarter)
     came_back = lax.all_to_all(answered, "ep", split_axis=0, concat_axis=0, tiled=True)

time: 145 us -> 153 us (1.055)
  Pallas kernels: 53.1 us -> 70.1 us
  waiting for transfers between devices: 62.5 us -> 52.5 us
  starting transfers between devices: 0.09 us -> 3.12 us
  other arithmetic: 6.45 us -> 4.02 us
    unnamed x4, waiting for transfers between devices: 16.8 us -> 0.74 us
    reduce_scatter x1 -> x2, waiting for transfers between devices: 38.4 us -> 49 us  [shards(): summed = lax.psum_scatter(answered, 'ep', scatter_dimension=0, tiled=True)]
    pallas_call x1 -> x2, Pallas kernels: 15 us -> 24.4 us  [hidden_units(): pl.pallas_call(hidden_kernel, grid=(width // tile,), in_specs=[pl.BlockSp...]
    all_gather x1 -> x2, waiting for transfers between devices: 7.29 us -> 0.55 us  [shards(): lax.all_gather(rows, 'ep', axis=0, tiled=True)]
    pallas_call x1 -> x2, Pallas kernels: 9.28 us -> 14.8 us  [project_down(): pl.pallas_call(project_kernel, grid=(pl.cdiv(model_width, tile),), in_spe...]
    reduce_sum x3 -> x0, other arithmetic: 3.02 us -> none  [the longest x1 1.16 us: rms_normed(): mean_square = jnp.mean(widened * widened, axis=-1, keepdims=True)]
    ppermute x0 -> x2, starting transfers between devices: none -> 3 us  [tp_sum(): lax.ppermute(sent, 'tp', [(k, (k + away) % tp_count) for k in range(tp_co...]
    ppermute x0 -> x2, waiting for transfers between devices: none -> 2.23 us  [tp_sum(): lax.ppermute(sent, 'tp', [(k, (k + away) % tp_count) for k in range(tp_co...]
  transfers between devices with their start and end apart: 3 -> 6, of which waited for: 3 -> 4; matrix products, arithmetic and copies ran while one was open for 3% -> 4% of each run, Pallas kernels for 20% -> 45%
where the time goes in v2:
time: 153 us; the launch traced here: 151 us
  Pallas kernels  70.1 us (46%)
  waiting for transfers between devices  52.5 us (34%)
  between operations  13.2 us (9%)
  local copies, waits for them, and re-layouts  8.41 us (5%)
  other arithmetic  4.02 us (3%)
  starting transfers between devices  3.12 us (2%)
    reduce_scatter x2, waiting for transfers between devices, shards(): summed = lax.psum_scatter(answered, 'ep', scatter_dimension=0, tiled=True)  49 us
    pallas_call x2, Pallas kernels, hidden_units(): pl.pallas_call(hidden_kernel, grid=(width // tile,), in_specs=[pl.BlockSp...  24.4 us
    pallas_call x1, Pallas kernels, unpack_gate_up(): pl.pallas_call(lambda *refs: gate_up_kernel(*refs, step=step, block_words...  17.7 us
    pallas_call x2, Pallas kernels, project_down(): pl.pallas_call(project_kernel, grid=(pl.cdiv(model_width, tile),), in_spe...  14.8 us
    pallas_call x1, Pallas kernels, unpack_down(): pl.pallas_call(down_kernel, grid=(word_count // step,), in_specs=[pl.Bloc...  11.2 us
    unnamed x7, local copies, waits for them, and re-layouts  4.85 us
  transfers between devices with their start and end apart: 6, of which 4 were waited for; matrix products, arithmetic and copies ran while one was open for 4% of the time, Pallas kernels for 45%

profile of v2, /device:TPU:0, one launch (start us, length us, event | category | flops | bytes accessed | tf_op | source)
XLA Modules:
  0.0 151.4 jit_solution(5938916460811835977)
XLA Ops:
  6.5 0.0 all-gather.3.cloned.1.call-start
  6.5 1.4 copy.11.refs_2_
  7.9 1.4 copy.12.refs_3_
  9.3 1.3 reshape.56.refs_1_
  10.6 2.1 %norm.1 = (bf16[32,2944]{1,0:T(8,128)(2,1)}, bf16[32,2944]{1,0:T(8,128)(2,1)}) custom-call(bf16[64,2880]{1,0:T(8,128)(2,1)} %refs_0_.1, bf16[1,2880]{1,0:T(2,128)(2,1)} %reshape.56.refs_1_, s32[64,4]{1,0:T(8,128)} %copy.11.refs_2_, f32[64,4]{1,0:T(8,128)} %copy.12.refs_3_), custom_call_target="tpu_custom_call" | custom-call | tf_op jit(solution)/shard_map/norm/pallas_call | solution.py:195
  12.7 0.0 all-gather.3.cloned.1.call-update
  12.8 0.0 all-gather.5.cloned.1.call-start
  12.8 0.7 all-gather.5.cloned.1.call-update
  13.5 0.0 reduce-scatter.3.cloned.1.call-start
  13.6 0.7 convert_element_type.32
  14.3 2.1 %copy.13 = bf16[1,40,2880]{1,2,0:T(8,128)(2,1)} copy(bf16[1,40,2880]{2,1,0:T(8,128)(2,1)} %param.18) | data formatting | bytes 460800 | tf_op args[8]
  16.4 11.2 %unpack_down.1.weight_ref = bf16[2880,1280]{1,0:T(8,128)(2,1)} custom-call(s32[360,1280]{1,0:T(8,128)} %bitcast.10, bf16[2880,40]{1,0:T(8,128)(2,1)} %bitcast.9), custom_call_target="tpu_custom_call" | custom-call | tf_op jit(solution)/shard_map/unpack_down/pallas_call | solution.py:93
  27.5 0.3 dynamic_update_slice.3.bias_ref
  27.8 0.0 copy-start.1
  27.8 17.7 %unpack_gate_up.1 = (bf16[2880,2560]{1,0:T(8,128)(2,1)}, f32[1,2560]{1,0:T(1,128)}) custom-call(s32[360,2560]{1,0:T(8,128)} %bitcast.8, bf16[90,2560]{1,0:T(8,128)(2,1)} %bitcast.11, bf16[1,2560]{1,0:T(2,128)(2,1)} %refs_2_.2), custom_call_target="tpu_custom_call" | custom-call | tf_op jit(solution)/shard_map/unpack_gate_up/pallas_call | solution.py:56
  45.5 0.0 copy-done.1
  45.5 0.5 and_convert_fusion.pick_ref
  46.1 0.0 all-gather.3.cloned.1.call-done.rows_ref.tail_ref
  46.1 12.1 %hidden_units.2.rows_ref = bf16[256,1280]{1,0:T(8,128)(2,1)} custom-call(bf16[256,2944]{1,0:T(8,128)(2,1)} %all-gather.3.cloned.1.call-done.rows_ref.tail_ref, bf16[2880,2560]{1,0:T(8,128)(2,1)} %get-tuple-element.10.weight_ref, f32[1,2560]{1,0:T(1,128)} %get-tuple-element.11.bias_ref), custom_call_target="tpu_custom_call" | custom-call | tf_op jit(solution)/shard_map/hidden_units/pallas_call | solution.py:121
  58.2 7.4 %project_down.2 = bf16[256,2880]{1,0:T(8,128)(2,1)} custom-call(bf16[256,1280]{1,0:T(8,128)(2,1)} %hidden_units.2.rows_ref, bf16[2880,1280]{1,0:T(8,128)(2,1)} %unpack_down.1.weight_ref, f32[1,2880]{1,0:T(1,128)} %copy-done.1, bf16[256,2944]{1,0:T(8,128)(2,1)} %all-gather.3.cloned.1.call-done.rows_ref.tail_ref, f32[1,128]{1,0:T(1,128)} %and_convert_fusion.pick_ref), custom_call_target="tpu_custom_call" | custom-call | tf_op jit(solution)/shard_map/project_down/pallas_call | solution.py:148
  65.6 0.0 reduce-scatter.3.cloned.1.call-update
  65.6 0.0 reduce-scatter.5.cloned.1.call-start
  65.7 0.6 all-gather.5.cloned.1.call-done.rows_ref.tail_ref
  66.2 12.2 %hidden_units.3.rows_ref = bf16[256,1280]{1,0:T(8,128)(2,1)} custom-call(bf16[256,2944]{1,0:T(8,128)(2,1)} %all-gather.5.cloned.1.call-done.rows_ref.tail_ref, bf16[2880,2560]{1,0:T(8,128)(2,1)} %get-tuple-element.10.weight_ref, f32[1,2560]{1,0:T(1,128)} %get-tuple-element.11.bias_ref), custom_call_target="tpu_custom_call" | custom-call | tf_op jit(solution)/shard_map/hidden_units/pallas_call | solution.py:121
  78.5 7.4 %project_down.3 = bf16[256,2880]{1,0:T(8,128)(2,1)} custom-call(bf16[256,1280]{1,0:T(8,128)(2,1)} %hidden_units.3.rows_ref, bf16[2880,1280]{1,0:T(8,128)(2,1)} %unpack_down.1.weight_ref, f32[1,2880]{1,0:T(1,128)} %copy-done.1, bf16[256,2944]{1,0:T(8,128)(2,1)} %all-gather.5.cloned.1.call-done.rows_ref.tail_ref, f32[1,128]{1,0:T(1,128)} %and_convert_fusion.pick_ref), custom_call_target="tpu_custom_call" | custom-call | tf_op jit(solution)/shard_map/project_down/pallas_call | solution.py:148
  85.8 0.0 copy-start
  85.8 0.0 reduce-scatter.5.cloned.1.call-update
  85.9 16.9 %reduce-scatter.3.cloned.1.call-done = bf16[32,2880]{1,0:T(8,128)(2,1)} async-done(((bf16[256,2880]{1,0:T(8,128)(2,1)}), bf16[32,2880]{1,0:T(8,128)(2,1)}) %reduce-scatter.3.cloned.1.call-update) | async-done | bytes 184336 | tf_op jit(solution)/shard_map/reduce_scatter | solution.py:262
  102.8 1.0 constant_dynamic-slice_fusion.1
  103.8 1.5 %collective-permute-start = (bf16[32,1440]{1,0:T(8,128)(2,1)S(1)}, bf16[32,1440]{1,0:T(8,128)(2,1)S(1)}, u32[]{:S(2)}, u32[]{:S(2)}) collective-permute-start(bf16[32,1440]{1,0:T(8,128)(2,1)S(1)} %constant_dynamic-slice_fusion.1), channel_id=1, source_target_pairs={{0,1},{1,0},{2,3},{3,2},{4,5},{5,4},{6,7},{7,6},{8,9},{9,8},{10,11... | collective-permute-start | bytes 276488 | tf_op jit(solution)/shard_map/ppermute | solution.py:215
  105.3 32.1 %reduce-scatter.5.cloned.1.call-done = bf16[32,2880]{1,0:T(8,128)(2,1)} async-done(((bf16[256,2880]{1,0:T(8,128)(2,1)}), bf16[32,2880]{1,0:T(8,128)(2,1)}) %reduce-scatter.5.cloned.1.call-update) | async-done | bytes 184336 | tf_op jit(solution)/shard_map/reduce_scatter | solution.py:262
  137.4 1.0 constant_dynamic-slice_fusion
  138.4 1.5 collective-permute-start.1
  139.9 0.0 collective-permute-done
  139.9 1.0 convert_add_fusion.1
  140.9 2.2 %collective-permute-done.1 = bf16[32,1440]{1,0:T(8,128)(2,1)S(1)} collective-permute-done((bf16[32,1440]{1,0:T(8,128)(2,1)S(1)}, bf16[32,1440]{1,0:T(8,128)(2,1)S(1)}, u32[]{:S(2)}, u32[]{:S(2)}) %collective-permute-start.1) | collective-permute-done | bytes 92192 | tf_op jit(solution)/shard_map/ppermute | solution.py:215
  143.1 1.0 convert_add_fusion
  144.1 0.0 copy-done
  144.1 0.8 fusion
  (1 shorter events, 0.0 us)
Async XLA Ops:
  6.5 39.5 %all-gather.3.cloned.1.call-start = ((), (), s32[]{:S(2)}) async-start(), calls=%async_computation.2 | async-start | bytes 1695744 | tf_op jit(solution)/shard_map/all_gather | solution.py:257
  12.8 53.5 %all-gather.5.cloned.1.call-start = ((), (), s32[]{:S(2)}) async-start(), calls=%async_computation.4 | async-start | bytes 1695744 | tf_op jit(solution)/shard_map/all_gather | solution.py:257
  13.5 89.3 %reduce-scatter.3.cloned.1.call-start = ((), (), s32[]{:S(2)}) async-start(), calls=%async_computation.3 | async-start | bytes 1695744 | tf_op jit(solution)/shard_map/reduce_scatter | solution.py:262
  27.8 17.7 %copy-start.1 = (f32[1,2880]{1,0:T(1,128)}, f32[1,2880]{1,0:T(1,128)S(1)}, u32[]{:S(2)}) copy-start(f32[1,2880]{1,0:T(1,128)S(1)} %dynamic_update_slice.3.bias_ref) | copy-start | bytes 34564
  65.6 71.8 %reduce-scatter.5.cloned.1.call-start = ((), (), s32[]{:S(2)}) async-start(), calls=%async_computation.5 | async-start | bytes 1695744 | tf_op jit(solution)/shard_map/reduce_scatter | solution.py:262
  85.8 58.2 %copy-start = (bf16[64,2880]{1,0:T(8,128)(2,1)S(1)}, bf16[64,2880]{1,0:T(8,128)(2,1)}, u32[]{:S(2)}) copy-start(bf16[64,2880]{1,0:T(8,128)(2,1)} %refs_0_.1) | copy-start | bytes 1105924
  103.8 36.1 %collective-permute-start = (bf16[32,1440]{1,0:T(8,128)(2,1)S(1)}, bf16[32,1440]{1,0:T(8,128)(2,1)S(1)}, u32[]{:S(2)}, u32[]{:S(2)}) collective-permute-start(bf16[32,1440]{1,0:T(8,128)(2,1)S(1)} %constant_dynamic-slice_fusion.1), channel_id=1, source_target_pairs={{0,1},{1,0},{2,3},{3,2},{4,5},{5,4},{6,7},{7,6},{8,9},{9,8},{10,11... | collective-permute-start | bytes 276488 | tf_op jit(solution)/shard_map/ppermute | solution.py:215
  138.4 4.7 %collective-permute-start.1 = (bf16[32,1440]{1,0:T(8,128)(2,1)S(1)}, bf16[32,1440]{1,0:T(8,128)(2,1)S(1)}, u32[]{:S(2)}, u32[]{:S(2)}) collective-permute-start(bf16[32,1440]{1,0:T(8,128)(2,1)S(1)} %constant_dynamic-slice_fusion), channel_id=1, source_target_pairs={{0,1},{1,0},{2,3},{3,2},{4,5},{5,4},{6,7},{7,6},{8,9},{9,8},{10,11... | collective-permute-start | bytes 276488 | tf_op jit(solution)/shard_map/ppermute | solution.py:215
Sparse Core Ops, SparseCore 0:
  12.9 27.5 all-gather.2
  42.1 24.0 all-gather.4
  68.5 34.2 reduce-scatter.2
  104.9 32.4 reduce-scatter.4

commit v3 on v2

--- a/solution.py
+++ b/solution.py
@@ -6,7 +6,9 @@
 from jax.sharding import PartitionSpec as P
 
 VMEM_BYTES = 56 * 1024 * 1024
-PIECES = 2
+PIECES = 1
+DOWN_TILE = 1536
+HIDDEN_STEP = 512
 
 
 def largest_step(total, limit, multiple):
@@ -104,29 +106,34 @@
     )(codes.T, scales.T)
 
 
-def hidden_kernel(rows_ref, weight_ref, bias_ref, out_ref):
+def hidden_kernel(rows_ref, weight_ref, bias_ref, out_ref, *, tile):
     model_width, width = weight_ref.shape
-    half = width // 2
-    projected = jnp.dot(
-        rows_ref[:, :model_width], weight_ref[...], preferred_element_type=jnp.float32
-    ) + bias_ref[...]
-    gate = jnp.minimum(projected[:, :half], 7.0)
-    upward = jnp.clip(projected[:, half:], -7.0, 7.0)
-    out_ref[...] = (gate * jax.nn.sigmoid(1.702 * gate) * (upward + 1.0)).astype(jnp.bfloat16)
+    half = tile // 2
+    for part in range(width // tile):
+        columns = slice(part * tile, (part + 1) * tile)
+        projected = jnp.dot(
+            rows_ref[:, :model_width], weight_ref[:, columns], preferred_element_type=jnp.float32
+        ) + bias_ref[:, columns]
+        gate = jnp.minimum(projected[:, :half], 7.0)
+        upward = jnp.clip(projected[:, half:], -7.0, 7.0)
+        out_ref[:, part * half : (part + 1) * half] = (
+            gate * jax.nn.sigmoid(1.702 * gate) * (upward + 1.0)
+        ).astype(jnp.bfloat16)
 
 
 def hidden_units(rows, weight, bias, tile):
     row_count = rows.shape[0]
     model_width, width = weight.shape
-    return pl.pallas_call(
-        hidden_kernel,
-        grid=(width // tile,),
+    step = largest_step(width, HIDDEN_STEP, tile)
+    return pl.pallas_call(
+        lambda *refs: hidden_kernel(*refs, tile=tile),
+        grid=(width // step,),
         in_specs=[
             pl.BlockSpec(rows.shape, lambda i: (0, 0)),
-            pl.BlockSpec((model_width, tile), lambda i: (0, i)),
-            pl.BlockSpec((1, tile), lambda i: (0, i)),
-        ],
-        out_specs=pl.BlockSpec((row_count, tile // 2), lambda i: (0, i)),
+            pl.BlockSpec((model_width, step), lambda i: (0, i)),
+            pl.BlockSpec((1, step), lambda i: (0, i)),
+        ],
+        out_specs=pl.BlockSpec((row_count, step // 2), lambda i: (0, i)),
         out_shape=jax.ShapeDtypeStruct((row_count, width // 2), jnp.bfloat16),
         compiler_params=pltpu.CompilerParams(vmem_limit_bytes=VMEM_BYTES),
         name="hidden_units",
@@ -144,7 +151,7 @@
 def project_down(rows, weight, bias, tail, pick):
     row_count, unit_count = rows.shape
     model_width = weight.shape[0]
-    tile = 512
+    tile = DOWN_TILE
     return pl.pallas_call(
         project_kernel,
         grid=(pl.cdiv(model_width, tile),),
@@ -162,7 +169,7 @@
     )(rows, weight, bias, tail, pick)
 
 
-def norm_kernel(hidden_ref, gain_ref, experts_ref, weight_ref, *out_refs, ep_count):
+def norm_kernel(hidden_ref, gain_ref, factor_ref, *out_refs, ep_count):
     tok_count, model_width = hidden_ref.shape
     total = out_refs[0].shape[1]
     widened = hidden_ref[...].astype(jnp.float32)
@@ -172,11 +179,7 @@
     )
     tail = total - model_width
     place = lax.broadcasted_iota(jnp.int32, (tok_count, tail), 1) - (tail - 3 * ep_count)
-    factor = jnp.zeros((tok_count, tail), jnp.float32)
-    for position in range(experts_ref.shape[1]):
-        chosen = experts_ref[:, position : position + 1]
-        named = (place == chosen) | (place == chosen + ep_count) | (place == chosen + 2 * ep_count)
-        factor = factor + jnp.where(named, weight_ref[:, position : position + 1], 0.0)
+    factor = factor_ref[...]
     upper = factor.astype(jnp.bfloat16).astype(jnp.float32)
     rest = factor - upper
     middle = rest.astype(jnp.bfloat16).astype(jnp.float32)
@@ -192,12 +195,17 @@
     tok_count, model_width = hidden.shape
     total = -(-(model_width + 3 * ep_count) // 128) * 128
     shape = jax.ShapeDtypeStruct((tok_count // pieces, total), jnp.bfloat16)
+    place = jnp.arange(total - model_width, dtype=jnp.int32) - (total - model_width - 3 * ep_count)
+    expert = jnp.where(place < 0, -1, place % ep_count)
+    factor = jnp.sum(
+        jnp.where(route_experts[:, :, None] == expert, route_weight[:, :, None], 0.0), axis=1
+    )
     return pl.pallas_call(
         lambda *refs: norm_kernel(*refs, ep_count=ep_count),
         out_shape=[shape] * pieces,
         compiler_params=pltpu.CompilerParams(vmem_limit_bytes=VMEM_BYTES),
         name="norm",
-    )(hidden, gain.reshape(1, -1), route_experts, route_weight)
+    )(hidden, gain.astype(jnp.float32).reshape(1, -1), factor)
 
 
 def rms_normed(hidden, norm_gain):
@@ -261,7 +269,7 @@
             answered = project_down(activated, down_weight, lower_bias, rows, pick)
             summed = lax.psum_scatter(answered, "ep", scatter_dimension=0, tiled=True)
             outputs.append(tp_sum(summed, tp_rank, tp_count, quarter))
-        summed = jnp.concatenate(outputs, axis=0)
+        summed = outputs[0] if PIECES == 1 else jnp.concatenate(outputs, axis=0)
         return (own_cols + summed).astype(jnp.bfloat16)
 
     normed = rms_normed(hidden, norm_gain)

time: 153 us -> 127 us (0.83)
  Pallas kernels: 70.1 us -> 52.1 us
  local copies, waits for them, and re-layouts: 8.41 us -> 4.74 us
  waiting for transfers between devices: 52.5 us -> 50.3 us
  starting transfers between devices: 3.12 us -> 1.55 us
    pallas_call x2 -> x1, Pallas kernels: 24.4 us -> 12.9 us  [hidden_units(): pl.pallas_call(lambda *refs: hidden_kernel(*refs, tile=tile), grid=(width...]
    reduce_scatter x2 -> x1, waiting for transfers between devices: 49 us -> 38.7 us  [shards(): summed = lax.psum_scatter(answered, 'ep', scatter_dimension=0, tiled=True)]
    all_gather x2 -> x1, waiting for transfers between devices: 0.55 us -> 7.33 us  [shards(): lax.all_gather(rows, 'ep', axis=0, tiled=True)]
    pallas_call x2 -> x1, Pallas kernels: 14.8 us -> 8.24 us  [project_down(): pl.pallas_call(project_kernel, grid=(pl.cdiv(model_width, tile),), in_spe...]
    unnamed x7 -> x5, local copies, waits for them, and re-layouts: 4.85 us -> 2.1 us
    ppermute x2 -> x1, waiting for transfers between devices: 2.23 us -> 4.23 us  [tp_sum(): lax.ppermute(sent, 'tp', [(k, (k + away) % tp_count) for k in range(tp_co...]
    add x2 -> x0, other arithmetic: 1.98 us -> none  [tp_sum(): summed = summed + got.astype(jnp.float32)]
  transfers between devices with their start and end apart: 6 -> 3, of which waited for: 4 -> 3; matrix products, arithmetic and copies ran while one was open for 4% -> 3% of each run, Pallas kernels for 45% -> 23%
where the time goes in v3:
time: 127 us
  Pallas kernels  52.1 us (41%)
  waiting for transfers between devices  50.3 us (40%)
  between operations  13.5 us (11%)
  local copies, waits for them, and re-layouts  4.74 us (4%)
  other arithmetic  4.48 us (4%)
  starting transfers between devices  1.55 us (1%)
    reduce_scatter x1, waiting for transfers between devices, shards(): summed = lax.psum_scatter(answered, 'ep', scatter_dimension=0, tiled=True)  38.7 us
    pallas_call x1, Pallas kernels, unpack_gate_up(): pl.pallas_call(lambda *refs: gate_up_kernel(*refs, step=step, block_words...  17.7 us
    pallas_call x1, Pallas kernels, hidden_units(): pl.pallas_call(lambda *refs: hidden_kernel(*refs, tile=tile), grid=(width...  12.9 us
    pallas_call x1, Pallas kernels, unpack_down(): pl.pallas_call(down_kernel, grid=(word_count // step,), in_specs=[pl.Bloc...  11.2 us
    pallas_call x1, Pallas kernels, project_down(): pl.pallas_call(project_kernel, grid=(pl.cdiv(model_width, tile),), in_spe...  8.24 us
    all_gather x1, waiting for transfers between devices, shards(): lax.all_gather(rows, 'ep', axis=0, tiled=True)  7.33 us
    ppermute x1, waiting for transfers between devices, tp_sum(): lax.ppermute(sent, 'tp', [(k, (k + away) % tp_count) for k in range(tp_co...  4.23 us
  transfers between devices with their start and end apart: 3, of which 3 were waited for; matrix products, arithmetic and copies ran while one was open for 3% of the time, Pallas kernels for 23%

profile of v3, /device:TPU:0, one launch (start us, length us, event | category | flops | bytes accessed | tf_op | source)
XLA Modules:
  0.0 126.6 jit_solution(7892611191371964617)
XLA Ops:
  6.5 0.0 all-gather.2.cloned.1.call-start
  6.5 1.3 %reshape.80.refs_1_ = f32[1,2880]{1,0:T(1,128)} reshape(bf16[2880]{0:T(1024)(128)(2,1)} %param.13) | data formatting | bytes 17280 | tf_op jit(solution)/shard_map/reshape | solution.py:208
  7.8 1.5 %select_reduce_fusion.refs_2_ = f32[64,64]{1,0:T(8,128)} fusion(f32[64,4]{0,1:T(4,128)} %param.12, s32[64]{0:T(128)S(1)} %compare_select_fusion.2, s32[64,4]{0,1:T(4,128)} %param.11), kind=kLoop, calls=%fused_computation.1 | loop fusion | flops 45056 | bytes 18688 | tf_op jit(solution)/shard_map/reduce_sum | solution.py:200
  9.3 2.0 %norm.1 = bf16[64,2944]{1,0:T(8,128)(2,1)} custom-call(bf16[64,2880]{1,0:T(8,128)(2,1)} %refs_0_.1, f32[1,2880]{1,0:T(1,128)} %reshape.80.refs_1_, f32[64,64]{1,0:T(8,128)} %select_reduce_fusion.refs_2_), custom_call_target="tpu_custom_call" | custom-call | tf_op jit(solution)/shard_map/norm/pallas_call | solution.py:203
  11.3 0.0 all-gather.2.cloned.1.call-update
  11.3 0.0 reduce-scatter.2.cloned.1.call-start
  11.4 2.1 %copy.14 = bf16[1,40,2880]{1,2,0:T(8,128)(2,1)} copy(bf16[1,40,2880]{2,1,0:T(8,128)(2,1)} %param.18) | data formatting | bytes 460800 | tf_op args[8]
  13.5 0.7 convert_element_type.27
  14.2 11.2 %unpack_down.1.weight_ref = bf16[2880,1280]{1,0:T(8,128)(2,1)} custom-call(s32[360,1280]{1,0:T(8,128)} %bitcast.10, bf16[2880,40]{1,0:T(8,128)(2,1)} %bitcast.9), custom_call_target="tpu_custom_call" | custom-call | tf_op jit(solution)/shard_map/unpack_down/pallas_call | solution.py:95
  25.3 17.7 %unpack_gate_up.1 = (bf16[2880,2560]{1,0:T(8,128)(2,1)}, f32[1,2560]{1,0:T(1,128)}) custom-call(s32[360,2560]{1,0:T(8,128)} %bitcast.8, bf16[90,2560]{1,0:T(8,128)(2,1)} %bitcast.11, bf16[1,2560]{1,0:T(2,128)(2,1)} %refs_2_.1), custom_call_target="tpu_custom_call" | custom-call | tf_op jit(solution)/shard_map/unpack_gate_up/pallas_call | solution.py:58
  43.1 0.3 dynamic_update_slice.3.bias_ref
  43.4 0.0 copy-start.1
  43.4 0.5 and_convert_fusion.pick_ref
  43.9 7.3 %all-gather.2.cloned.1.call-done.refs_0_.tail_ref = bf16[512,2944]{1,0:T(8,128)(2,1)} async-done(((bf16[64,2944]{1,0:T(8,128)(2,1)}), bf16[512,2944]{1,0:T(8,128)(2,1)}) %all-gather.2.cloned.1.call-update) | async-done | bytes 3014672 | tf_op jit(solution)/shard_map/all_gather | solution.py:265
  51.3 12.9 %hidden_units.1.rows_ref = bf16[512,1280]{1,0:T(8,128)(2,1)} custom-call(bf16[512,2944]{1,0:T(8,128)(2,1)} %all-gather.2.cloned.1.call-done.refs_0_.tail_ref, bf16[2880,2560]{1,0:T(8,128)(2,1)} %get-tuple-element.7.refs_1_, f32[1,2560]{1,0:T(1,128)} %get-tuple-element.8.refs_2_), custom_call_target="tpu_custom_call" | custom-call | tf_op jit(solution)/shard_map/hidden_units/pallas_call | solution.py:128
  64.2 0.0 copy-done.1
  64.2 8.2 %project_down.1 = bf16[512,2880]{1,0:T(8,128)(2,1)} custom-call(bf16[512,1280]{1,0:T(8,128)(2,1)} %hidden_units.1.rows_ref, bf16[2880,1280]{1,0:T(8,128)(2,1)} %unpack_down.1.weight_ref, f32[1,2880]{1,0:T(1,128)} %copy-done.1, bf16[512,2944]{1,0:T(8,128)(2,1)} %all-gather.2.cloned.1.call-done.refs_0_.tail_ref, f32[1,128]{1,0:T(1,128)} %and_convert_fusion.pick_ref), custom_call_target="tpu_custom_call" | custom-call | tf_op jit(solution)/shard_map/project_down/pallas_call | solution.py:155
  72.5 0.0 copy-start
  72.5 0.0 reduce-scatter.2.cloned.1.call-update
  72.5 38.7 %reduce-scatter.2.cloned.1.call-done = bf16[64,2880]{1,0:T(8,128)(2,1)} async-done(((bf16[512,2880]{1,0:T(8,128)(2,1)}), bf16[64,2880]{1,0:T(8,128)(2,1)}) %reduce-scatter.2.cloned.1.call-update) | async-done | bytes 368656 | tf_op jit(solution)/shard_map/reduce_scatter | solution.py:270
  111.2 1.0 constant_dynamic-slice_fusion
  112.2 1.5 %collective-permute-start = (bf16[64,1440]{1,0:T(8,128)(2,1)S(1)}, bf16[64,1440]{1,0:T(8,128)(2,1)S(1)}, u32[]{:S(2)}, u32[]{:S(2)}) collective-permute-start(bf16[64,1440]{1,0:T(8,128)(2,1)S(1)} %constant_dynamic-slice_fusion), channel_id=1, source_target_pairs={{0,1},{1,0},{2,3},{3,2},{4,5},{5,4},{6,7},{7,6},{8,9},{9,8},{10,11... | collective-permute-start | bytes 552968 | tf_op jit(solution)/shard_map/ppermute | solution.py:223
  113.7 4.2 %collective-permute-done = bf16[64,1440]{1,0:T(8,128)(2,1)S(1)} collective-permute-done((bf16[64,1440]{1,0:T(8,128)(2,1)S(1)}, bf16[64,1440]{1,0:T(8,128)(2,1)S(1)}, u32[]{:S(2)}, u32[]{:S(2)}) %collective-permute-start) | collective-permute-done | bytes 184352 | tf_op jit(solution)/shard_map/ppermute | solution.py:223
  118.0 0.0 copy-done
  118.0 1.8 %add_convert_fusion = bf16[64,1440]{1,0:T(8,128)(2,1)} fusion(bf16[64,1440]{1,0:T(8,128)(2,1)S(1)} %collective-permute-done, bf16[64,2880]{1,0:T(8,128)(2,1)} %reduce-scatter.2.cloned.1.call-done, s32[]{:T(128)S(6)} %select_n.50, bf16[64,2880]{1,0:T(8,128)(2,1)S(1)} %copy-done), kind=kLoop, calls=%fused_computation | loop fusion | flops 552960 | bytes 737284 | tf_op jit(solution)/shard_map/convert_element_type | solution.py:273
  (2 shorter events, 0.0 us)
Async XLA Ops:
  6.5 44.7 %all-gather.2.cloned.1.call-start = ((), (), s32[]{:S(2)}) async-start(), calls=%async_computation.1 | async-start | bytes 3391488 | tf_op jit(solution)/shard_map/all_gather | solution.py:265
  11.3 99.9 %reduce-scatter.2.cloned.1.call-start = ((), (), s32[]{:S(2)}) async-start(), calls=%async_computation.2 | async-start | bytes 3391488 | tf_op jit(solution)/shard_map/reduce_scatter | solution.py:270
  43.4 20.8 %copy-start.1 = (f32[1,2880]{1,0:T(1,128)}, f32[1,2880]{1,0:T(1,128)S(1)}, u32[]{:S(2)}) copy-start(f32[1,2880]{1,0:T(1,128)S(1)} %dynamic_update_slice.3.bias_ref) | copy-start | bytes 34564
  72.5 45.5 %copy-start = (bf16[64,2880]{1,0:T(8,128)(2,1)S(1)}, bf16[64,2880]{1,0:T(8,128)(2,1)}, u32[]{:S(2)}) copy-start(bf16[64,2880]{1,0:T(8,128)(2,1)} %refs_0_.1) | copy-start | bytes 1105924
  112.2 5.7 %collective-permute-start = (bf16[64,1440]{1,0:T(8,128)(2,1)S(1)}, bf16[64,1440]{1,0:T(8,128)(2,1)S(1)}, u32[]{:S(2)}, u32[]{:S(2)}) collective-permute-start(bf16[64,1440]{1,0:T(8,128)(2,1)S(1)} %constant_dynamic-slice_fusion), channel_id=1, source_target_pairs={{0,1},{1,0},{2,3},{3,2},{4,5},{5,4},{6,7},{7,6},{8,9},{9,8},{10,11... | collective-permute-start | bytes 552968 | tf_op jit(solution)/shard_map/ppermute | solution.py:223
Sparse Core Ops, SparseCore 0:
  11.4 39.7 all-gather.1
  72.6 38.5 reduce-scatter.1

commit v4 on v3

--- a/solution.py
+++ b/solution.py
@@ -174,7 +174,7 @@
     total = out_refs[0].shape[1]
     widened = hidden_ref[...].astype(jnp.float32)
     mean_square = jnp.mean(widened * widened, axis=-1, keepdims=True)
-    normed = (widened * lax.rsqrt(mean_square + 1e-05) * gain_ref[...].astype(jnp.float32)).astype(
+    normed = (widened * lax.rsqrt(mean_square + 1e-05) * gain_ref[...].astype(jnp.float32)[None, :]).astype(
         jnp.bfloat16
     )
     tail = total - model_width
@@ -205,7 +205,7 @@
         out_shape=[shape] * pieces,
         compiler_params=pltpu.CompilerParams(vmem_limit_bytes=VMEM_BYTES),
         name="norm",
-    )(hidden, gain.astype(jnp.float32).reshape(1, -1), factor)
+    )(hidden, gain, factor)
 
 
 def rms_normed(hidden, norm_gain):

time: 127 us -> 126 us (level)
  local copies, waits for them, and re-layouts: 4.74 us -> 3.44 us
    reshape x1 -> x0, local copies, waits for them, and re-layouts: 1.3 us -> none  [normed_with_factors(): gain.astype(jnp.float32).reshape(1, -1)]
where the time goes in v4:
time: 126 us; the launch traced here: 125 us
  Pallas kernels  52.1 us (41%)
  waiting for transfers between devices  50 us (40%)
  between operations  13.5 us (11%)
  other arithmetic  4.48 us (4%)
  local copies, waits for them, and re-layouts  3.44 us (3%)
  starting transfers between devices  1.72 us (1%)
    reduce_scatter x1, waiting for transfers between devices, shards(): summed = lax.psum_scatter(answered, 'ep', scatter_dimension=0, tiled=True)  38.5 us
    pallas_call x1, Pallas kernels, unpack_gate_up(): pl.pallas_call(lambda *refs: gate_up_kernel(*refs, step=step, block_words...  17.7 us
    pallas_call x1, Pallas kernels, hidden_units(): pl.pallas_call(lambda *refs: hidden_kernel(*refs, tile=tile), grid=(width...  12.9 us
    pallas_call x1, Pallas kernels, unpack_down(): pl.pallas_call(down_kernel, grid=(word_count // step,), in_specs=[pl.Bloc...  11.2 us
    pallas_call x1, Pallas kernels, project_down(): pl.pallas_call(project_kernel, grid=(pl.cdiv(model_width, tile),), in_spe...  8.25 us
    all_gather x1, waiting for transfers between devices, shards(): lax.all_gather(rows, 'ep', axis=0, tiled=True)  7.33 us
    ppermute x1, waiting for transfers between devices, tp_sum(): lax.ppermute(sent, 'tp', [(k, (k + away) % tp_count) for k in range(tp_co...  4.06 us
  transfers between devices with their start and end apart: 3, of which 3 were waited for; matrix products, arithmetic and copies ran while one was open for 3% of the time, Pallas kernels for 23%

profile of v4, /device:TPU:0, one launch (start us, length us, event | category | flops | bytes accessed | tf_op | source)
XLA Modules:
  0.0 125.2 jit_solution(16506384943974578118)
XLA Ops:
  6.5 0.0 all-gather.2.cloned.1.call-start
  6.5 1.5 %select_reduce_fusion.refs_2_ = f32[64,64]{1,0:T(8,128)} fusion(f32[64,4]{0,1:T(4,128)} %param.12, s32[64]{0:T(128)S(1)} %compare_select_fusion.2, s32[64,4]{0,1:T(4,128)} %param.11), kind=kLoop, calls=%fused_computation.1 | loop fusion | flops 45056 | bytes 18688 | tf_op jit(solution)/shard_map/reduce_sum | solution.py:200
  8.0 2.0 %norm.1 = bf16[64,2944]{1,0:T(8,128)(2,1)} custom-call(bf16[64,2880]{1,0:T(8,128)(2,1)} %refs_0_.1, bf16[2880]{0:T(1024)(128)(2,1)} %refs_1_.1, f32[64,64]{1,0:T(8,128)} %select_reduce_fusion.refs_2_), custom_call_target="tpu_custom_call" | custom-call | tf_op jit(solution)/shard_map/norm/pallas_call | solution.py:203
  10.0 0.0 all-gather.2.cloned.1.call-update
  10.0 0.0 reduce-scatter.2.cloned.1.call-start
  10.1 2.1 %copy.14 = bf16[1,40,2880]{1,2,0:T(8,128)(2,1)} copy(bf16[1,40,2880]{2,1,0:T(8,128)(2,1)} %param.18) | data formatting | bytes 460800 | tf_op args[8]
  12.2 0.7 convert_element_type.26
  12.9 11.2 %unpack_down.1.weight_ref = bf16[2880,1280]{1,0:T(8,128)(2,1)} custom-call(s32[360,1280]{1,0:T(8,128)} %bitcast.10, bf16[2880,40]{1,0:T(8,128)(2,1)} %bitcast.9), custom_call_target="tpu_custom_call" | custom-call | tf_op jit(solution)/shard_map/unpack_down/pallas_call | solution.py:95
  24.0 17.7 %unpack_gate_up.1 = (bf16[2880,2560]{1,0:T(8,128)(2,1)}, f32[1,2560]{1,0:T(1,128)}) custom-call(s32[360,2560]{1,0:T(8,128)} %bitcast.8, bf16[90,2560]{1,0:T(8,128)(2,1)} %bitcast.11, bf16[1,2560]{1,0:T(2,128)(2,1)} %refs_2_.1), custom_call_target="tpu_custom_call" | custom-call | tf_op jit(solution)/shard_map/unpack_gate_up/pallas_call | solution.py:58
  41.8 0.3 dynamic_update_slice.3.bias_ref
  42.1 0.0 copy-start.1
  42.1 0.5 and_convert_fusion.pick_ref
  42.6 7.3 %all-gather.2.cloned.1.call-done.refs_0_.tail_ref = bf16[512,2944]{1,0:T(8,128)(2,1)} async-done(((bf16[64,2944]{1,0:T(8,128)(2,1)}), bf16[512,2944]{1,0:T(8,128)(2,1)}) %all-gather.2.cloned.1.call-update) | async-done | bytes 3014672 | tf_op jit(solution)/shard_map/all_gather | solution.py:265
  50.0 12.9 %hidden_units.1.rows_ref = bf16[512,1280]{1,0:T(8,128)(2,1)} custom-call(bf16[512,2944]{1,0:T(8,128)(2,1)} %all-gather.2.cloned.1.call-done.refs_0_.tail_ref, bf16[2880,2560]{1,0:T(8,128)(2,1)} %get-tuple-element.7.refs_1_, f32[1,2560]{1,0:T(1,128)} %get-tuple-element.8.refs_2_), custom_call_target="tpu_custom_call" | custom-call | tf_op jit(solution)/shard_map/hidden_units/pallas_call | solution.py:128
  62.9 0.0 copy-done.1
  62.9 8.2 %project_down.1 = bf16[512,2880]{1,0:T(8,128)(2,1)} custom-call(bf16[512,1280]{1,0:T(8,128)(2,1)} %hidden_units.1.rows_ref, bf16[2880,1280]{1,0:T(8,128)(2,1)} %unpack_down.1.weight_ref, f32[1,2880]{1,0:T(1,128)} %copy-done.1, bf16[512,2944]{1,0:T(8,128)(2,1)} %all-gather.2.cloned.1.call-done.refs_0_.tail_ref, f32[1,128]{1,0:T(1,128)} %and_convert_fusion.pick_ref), custom_call_target="tpu_custom_call" | custom-call | tf_op jit(solution)/shard_map/project_down/pallas_call | solution.py:155
  71.2 0.0 copy-start
  71.2 0.0 reduce-scatter.2.cloned.1.call-update
  71.2 38.5 %reduce-scatter.2.cloned.1.call-done = bf16[64,2880]{1,0:T(8,128)(2,1)} async-done(((bf16[512,2880]{1,0:T(8,128)(2,1)}), bf16[64,2880]{1,0:T(8,128)(2,1)}) %reduce-scatter.2.cloned.1.call-update) | async-done | bytes 368656 | tf_op jit(solution)/shard_map/reduce_scatter | solution.py:270
  109.7 1.0 constant_dynamic-slice_fusion
  110.8 1.7 %collective-permute-start = (bf16[64,1440]{1,0:T(8,128)(2,1)S(1)}, bf16[64,1440]{1,0:T(8,128)(2,1)S(1)}, u32[]{:S(2)}, u32[]{:S(2)}) collective-permute-start(bf16[64,1440]{1,0:T(8,128)(2,1)S(1)} %constant_dynamic-slice_fusion), channel_id=1, source_target_pairs={{0,1},{1,0},{2,3},{3,2},{4,5},{5,4},{6,7},{7,6},{8,9},{9,8},{10,11... | collective-permute-start | bytes 552968 | tf_op jit(solution)/shard_map/ppermute | solution.py:223
  112.5 4.1 %collective-permute-done = bf16[64,1440]{1,0:T(8,128)(2,1)S(1)} collective-permute-done((bf16[64,1440]{1,0:T(8,128)(2,1)S(1)}, bf16[64,1440]{1,0:T(8,128)(2,1)S(1)}, u32[]{:S(2)}, u32[]{:S(2)}) %collective-permute-start) | collective-permute-done | bytes 184352 | tf_op jit(solution)/shard_map/ppermute | solution.py:223
  116.5 0.0 copy-done
  116.5 1.8 %add_convert_fusion = bf16[64,1440]{1,0:T(8,128)(2,1)} fusion(bf16[64,1440]{1,0:T(8,128)(2,1)S(1)} %collective-permute-done, bf16[64,2880]{1,0:T(8,128)(2,1)} %reduce-scatter.2.cloned.1.call-done, s32[]{:T(128)S(6)} %select_n.50, bf16[64,2880]{1,0:T(8,128)(2,1)S(1)} %copy-done), kind=kLoop, calls=%fused_computation | loop fusion | flops 552960 | bytes 737284 | tf_op jit(solution)/shard_map/convert_element_type | solution.py:273
  (2 shorter events, 0.0 us)
Async XLA Ops:
  6.5 43.4 %all-gather.2.cloned.1.call-start = ((), (), s32[]{:S(2)}) async-start(), calls=%async_computation.1 | async-start | bytes 3391488 | tf_op jit(solution)/shard_map/all_gather | solution.py:265
  10.0 99.7 %reduce-scatter.2.cloned.1.call-start = ((), (), s32[]{:S(2)}) async-start(), calls=%async_computation.2 | async-start | bytes 3391488 | tf_op jit(solution)/shard_map/reduce_scatter | solution.py:270
  42.1 20.8 %copy-start.1 = (f32[1,2880]{1,0:T(1,128)}, f32[1,2880]{1,0:T(1,128)S(1)}, u32[]{:S(2)}) copy-start(f32[1,2880]{1,0:T(1,128)S(1)} %dynamic_update_slice.3.bias_ref) | copy-start | bytes 34564
  71.2 45.4 %copy-start = (bf16[64,2880]{1,0:T(8,128)(2,1)S(1)}, bf16[64,2880]{1,0:T(8,128)(2,1)}, u32[]{:S(2)}) copy-start(bf16[64,2880]{1,0:T(8,128)(2,1)} %refs_0_.1) | copy-start | bytes 1105924
  110.8 5.7 %collective-permute-start = (bf16[64,1440]{1,0:T(8,128)(2,1)S(1)}, bf16[64,1440]{1,0:T(8,128)(2,1)S(1)}, u32[]{:S(2)}, u32[]{:S(2)}) collective-permute-start(bf16[64,1440]{1,0:T(8,128)(2,1)S(1)} %constant_dynamic-slice_fusion), channel_id=1, source_target_pairs={{0,1},{1,0},{2,3},{3,2},{4,5},{5,4},{6,7},{7,6},{8,9},{9,8},{10,11... | collective-permute-start | bytes 552968 | tf_op jit(solution)/shard_map/ppermute | solution.py:223
Sparse Core Ops, SparseCore 0:
  10.2 39.7 all-gather.1
  71.3 38.3 reduce-scatter.1
